TPU v7x, 512 devices: a whole 4x4x16 slice. The times are simulated.
512 devices in a mesh: prow: 16 (over y, x), pcol: 32 (over z, core).
Axes of the slice: x: 4, y: 4, z: 16, core: 2. Of those that a mesh axis runs over, the one named last changes fastest.
Arguments:
- schur: float32 [4, 16, 128, 2, 32, 128], P(None, 'prow', None, None, 'pcol'), may hold values from -0.0625 to 0.0625
- panel_inverse: float32 [2, 32, 128, 2, 16, 128], P(None, 'pcol', None, None, 'prow'), may hold values from -0.09375 to 0.09375
- coupling: float32 [4, 16, 128, 256], P(None, 'prow'), may hold values from -6 to 6
- zslab: float32 [4, 16, 128, 2, 32, 128], P(None, 'prow', None, None, 'pcol')
- targets: int32 [128], replicated, may hold values from 0 to 254
- pair_flags: int32 [128], replicated, may hold values 0 or 1
Outputs:
- eigenvectors: float32 [4, 16, 128, 128], P(None, 'prow', 'pcol')
All inputs are finite; a program needn't handle non-finite values.
Results may differ from a plain program's by a relative error of at most 0.0001.
Values sent between devices are 32-bit elements; how exact they have to be, the bound alone decides.
No kernel may reach another device: no remote copies, remote signals or barrier semaphores. Data moves between devices by JAX's collectives and lax.ppermute only.
A program may use at most 64 MiB of HBM per device.

v0:
```python
import jax
import jax.numpy as jnp
from jax import lax
from jax.sharding import Mesh
from jax.sharding import PartitionSpec as P

PCOL = ("pcol_0", "pcol_1")
PROW = ("prow_0", "prow_1")


EPSILON = 1e-06


def filled_up(lines, size):
    spare = -lines.shape[0] % size
    if not spare:
        return lines
    return jnp.concatenate([lines, jnp.zeros((spare, *lines.shape[1:]), lines.dtype)])


def from_everyone(value, axis):
    size = lax.axis_size(axis)
    return lax.all_to_all(
        jnp.broadcast_to(value[None], (size, *value.shape)), axis, 0, 0, tiled=True
    )


def in_order(pieces, dim):
    pieces = jnp.moveaxis(pieces, 0, dim)
    dims = pieces.shape
    return pieces.reshape(*dims[:dim], dims[dim] * dims[dim + 1], *dims[dim + 2 :])


def gather_directly(value, axis, dim):
    pieces = from_everyone(value, axis)
    return in_order(pieces, dim)


def split_up(value, dim, size):
    dims = value.shape
    pieces = value.reshape(*dims[:dim], size, dims[dim] // size, *dims[dim + 1 :])
    return jnp.moveaxis(pieces, dim, 0)


def sent_and_summed(value, axis, dim):
    size = lax.axis_size(axis)
    pieces = lax.all_to_all(split_up(value, dim, size), axis, 0, 0, tiled=True)
    return jnp.sum(pieces, axis=0)


def sum_by_parts(value, axes):
    lines = value.reshape(-1, value.shape[-1])
    padded = filled_up(lines, lax.axis_size(axes))
    whole = gather_directly(sent_and_summed(padded, axes, 0), axes, 0)
    return lax.slice_in_dim(whole, 0, len(lines)).reshape(value.shape)


def over_copies(value, axis):
    everything = from_everyone(value, axis)
    return jnp.sum(everything, axis=0)


def one_axis_at_a_time(value, axes):
    far, near = axes
    nearer = over_copies(value, near)
    return over_copies(nearer, far)


def shards(schur, panel_inverse, coupling, zslab, targets, pair_flags):
    block_size = schur.shape[2]
    row_blocks = schur.shape[0]
    col_blocks = schur.shape[3]
    ratio_rows = panel_inverse.shape[3]
    window = coupling.shape[3]
    vector_count = targets.shape[0]
    zrow_blocks = zslab.shape[0]
    panel_rows = ratio_rows * block_size
    triangle = schur.reshape(row_blocks * block_size, col_blocks * block_size)
    inverse = panel_inverse.reshape(col_blocks, block_size, panel_rows)
    strip_rows = coupling.reshape(row_blocks * block_size, window)
    z_rows = zslab.reshape(zrow_blocks * block_size, col_blocks * block_size)
    columns = jnp.arange(window, dtype=jnp.int32)[:, None]
    selection = (columns == targets[None, :]).astype(jnp.float32) + pair_flags[None, :].astype(
        jnp.float32
    ) * (columns == targets[None, :] + 1).astype(jnp.float32)
    right_side = -jnp.dot(strip_rows, selection, precision=lax.Precision.HIGHEST)
    pieces = [None] * col_blocks
    for panel_index in reversed(range(col_blocks)):
        residual = right_side[panel_index * panel_rows : (panel_index + 1) * panel_rows]
        if panel_index < col_blocks - 1:
            later_rows = jnp.concatenate(pieces[panel_index + 1 :], axis=0)
            partial_value = jnp.dot(
                triangle[
                    panel_index * panel_rows : (panel_index + 1) * panel_rows,
                    (panel_index + 1) * block_size :,
                ],
                later_rows,
                precision=lax.Precision.HIGHEST,
            )
            residual = residual - sum_by_parts(partial_value, PCOL)
        applied = jnp.dot(inverse[panel_index], residual, precision=lax.Precision.HIGHEST)
        pieces[panel_index] = over_copies(applied, PROW)
    transformed = jnp.dot(z_rows, jnp.concatenate(pieces, axis=0), precision=lax.Precision.HIGHEST)
    stacked = transformed.reshape(zrow_blocks, 1, block_size, vector_count)
    total_rows = zrow_blocks * block_size * lax.axis_size(PROW)
    owned_rows = sent_and_summed(stacked, PCOL, 2)
    squares = one_axis_at_a_time(
        jnp.sum(owned_rows * owned_rows, axis=(0, 1, 2)),
        (("prow_0", "prow_1"), ("pcol_0", "pcol_1")),
    )
    divisor = jnp.sqrt(squares / total_rows + EPSILON)
    return owned_rows / divisor[None, None, None, :]


def solution(mesh):
    split = Mesh(mesh.devices.reshape(4, 4, 16, 2), ("prow_0", "prow_1", "pcol_0", "pcol_1"))
    placed = (
        P(None, PROW, None, None, PCOL, None),
        P(None, PCOL, None, None, PROW, None),
        P(None, PROW, None, None),
        P(None, PROW, None, None, PCOL, None),
        P(),
        P(),
    )
    return jax.shard_map(
        shards, mesh=split, in_specs=placed, out_specs=P(None, PROW, PCOL, None), check_vma=False
    )
```

profile of v0, /device:TPU:1, one launch (start us, length us, event | category | flops | bytes accessed | tf_op | source)
XLA Modules:
  0.0 157.1 jit_solution(12456061616648821154)
XLA Ops:
  0.0 0.0 copy-start
  0.0 0.7 broadcast_add_fusion
  0.7 0.0 copy-done.4
  0.7 1.8 %slice_reduce_fusion = (f32[128,2,128]{2,1,0:T(2,128)S(1)}, f32[128,2,128]{2,1,0:T(2,128)S(1)}) fusion(f32[2,1,128,2,1,128]{5,4,3,2,1,0:T(1,128)} %param.7), kind=kLoop, calls=%fused_computation.19 | loop fusion | bytes 524288 | tf_op jit(solution)/shard_map/slice | solution.py:101
  2.5 0.0 copy-done
  2.5 0.0 copy-start.3
  2.6 0.6 copy-done.3
  3.2 0.7 fusion
  3.9 0.3 convolution_bitcast_fusion.3
  4.2 0.1 copy.26
  4.3 1.1 broadcast_in_dim.10
  5.4 7.7 %all-to-all-start = ((f32[16,128,128]{2,1,0:T(8,128)}), f32[16,128,128]{2,1,0:T(8,128)S(1)}, u32[]{:S(2)}, u32[]{:S(2)}) async-start(f32[16,128,128]{2,1,0:T(8,128)} %broadcast_in_dim.10), calls=%async_computation | async-start | bytes 2097152 | tf_op jit(solution)/shard_map/all_to_all | solution.py:23
  13.2 14.6 %all-to-all-done = f32[16,128,128]{2,1,0:T(8,128)S(1)} async-done(((f32[16,128,128]{2,1,0:T(8,128)}), f32[16,128,128]{2,1,0:T(8,128)S(1)}, u32[]{:S(2)}, u32[]{:S(2)}) %all-to-all-start) | async-done | bytes 1048608 | tf_op jit(solution)/shard_map/all_to_all | solution.py:23
  27.7 0.1 reduce_sum.65
  27.8 0.3 convolution_bitcast_fusion.1
  28.1 0.1 copy.27
  28.2 34.9 %all_to_all.37 = f32[32,8,128]{2,1,0:T(8,128)S(1)} all-to-all(f32[32,8,128]{2,1,0:T(8,128)S(1)} %bitcast.50), channel_id=1, replica_groups=mesh['prow_0'=4,'prow_1'=4,'pcol_0'=16,'pcol_1'=2] {'pcol_0','pcol_1'}, dimensions={0} | all-to-all | bytes 262144 | tf_op jit(solution)/shard_map/all_to_all | solution.py:47
  63.2 20.4 %all_to_all.38 = f32[32,8,128]{2,1,0:T(8,128)S(1)} all-to-all(f32[32,8,128]{2,1,0:T(8,128)S(1)} %broadcast_in_dim.11), channel_id=1, replica_groups=mesh['prow_0'=4,'prow_1'=4,'pcol_0'=16,'pcol_1'=2] {'pcol_0','pcol_1'}, dimensions={0} | all-to-all | bytes 262144 | tf_op jit(solution)/shard_map/all_to_all | solution.py:23
  83.6 0.1 copy.28
  83.7 0.3 convolution_bitcast_fusion.2
  83.9 0.1 copy.29
  84.0 0.1 broadcast_in_dim.12
  84.1 18.6 %all_to_all.39 = f32[16,128,128]{2,1,0:T(8,128)S(1)} all-to-all(f32[16,128,128]{2,1,0:T(8,128)S(1)} %broadcast_in_dim.12), channel_id=1, replica_groups=mesh['prow_0'=4,'prow_1'=4,'pcol_0'=16,'pcol_1'=2] {'prow_0','prow_1'}, dimensions={0} | all-to-all | bytes 2097152 | tf_op jit(solution)/shard_map/all_to_all | solution.py:23
  102.7 0.1 reduce_sum.67
  102.8 1.0 copy-done.1
  103.8 0.7 convolution_bitcast_fusion
  104.5 0.1 copy.30
  104.7 27.4 %all_to_all.40 = f32[32,4,1,4,128]{4,3,1,2,0:T(4,128)S(1)} all-to-all(f32[32,4,1,4,128]{4,3,1,2,0:T(4,128)S(1)} %copy.31), channel_id=1, replica_groups=mesh['prow_0'=4,'prow_1'=4,'pcol_0'=16,'pcol_1'=2] {'pcol_0','pcol_1'}, dimensions={0} | all-to-all | bytes 524288 | tf_op jit(solution)/shard_map/all_to_all | solution.py:47
  132.1 0.1 reduce_sum.68
  132.2 15.2 %all_to_all.41 = f32[32,1,128]{2,1,0:T(1,128)S(1)} all-to-all(f32[32,1,128]{2,1,0:T(1,128)S(1)} %broadcast_in_dim.13), channel_id=1, replica_groups=mesh['prow_0'=4,'prow_1'=4,'pcol_0'=16,'pcol_1'=2] {'pcol_0','pcol_1'}, dimensions={0} | all-to-all | bytes 32768 | tf_op jit(solution)/shard_map/all_to_all | solution.py:23
  147.4 9.0 %all_to_all.42 = f32[16,1,128]{2,1,0:T(1,128)S(1)} all-to-all(f32[16,1,128]{2,1,0:T(1,128)S(1)} %broadcast_in_dim.14), channel_id=1, replica_groups=mesh['prow_0'=4,'prow_1'=4,'pcol_0'=16,'pcol_1'=2] {'prow_0','prow_1'}, dimensions={0} | all-to-all | bytes 16384 | tf_op jit(solution)/shard_map/all_to_all | solution.py:23
  156.5 0.6 bitcast_divide_fusion
  (15 shorter events, 0.2 us)
Async XLA Ops:
  0.0 2.5 %copy-start = (f32[4,1,128,256]{3,2,1,0:T(8,128)S(1)}, f32[4,1,128,256]{3,2,1,0:T(8,128)}, u32[]{:S(2)}) copy-start(f32[4,1,128,256]{3,2,1,0:T(8,128)} %param.8) | copy-start | bytes 1572868
  0.0 0.7 copy-start.4
  2.5 0.7 copy-start.3
  5.4 7.7 %copy-start.2 = (f32[4,1,128,2,1,128]{5,4,3,2,1,0:T(1,128)S(1)}, f32[4,1,128,2,1,128]{5,4,3,2,1,0:T(1,128)}, u32[]{:S(2)}) copy-start(f32[4,1,128,2,1,128]{5,4,3,2,1,0:T(1,128)} %param.6) | copy-start | bytes 1572868
  5.4 22.3 %all-to-all-start = ((f32[16,128,128]{2,1,0:T(8,128)}), f32[16,128,128]{2,1,0:T(8,128)S(1)}, u32[]{:S(2)}, u32[]{:S(2)}) async-start(f32[16,128,128]{2,1,0:T(8,128)} %broadcast_in_dim.10), calls=%async_computation | async-start | bytes 2097152 | tf_op jit(solution)/shard_map/all_to_all | solution.py:23
  102.7 1.0 copy-start.1
where the time goes:
time: 158 us; the launch traced here: 157 us
  blocking collectives  126 us (80%)
  waiting for transfers between devices  14.6 us (9%)
  starting transfers between devices  7.71 us (5%)
  local copies, waits for them, and re-layouts  5.23 us (3%)
  matrix products  2.29 us (1%)
  other arithmetic  1.63 us (1%)
    all_to_all x4, blocking collectives, from_everyone(): lax.all_to_all(jnp.broadcast_to(value[None], (size, *value.shape)), axis,...  63.2 us
    all_to_all x2, blocking collectives, sent_and_summed(): pieces = lax.all_to_all(split_up(value, dim, size), axis, 0, 0, tiled=True)  62.3 us
    all_to_all x1, waiting for transfers between devices, from_everyone(): lax.all_to_all(jnp.broadcast_to(value[None], (size, *value.shape)), axis,...  14.6 us
    all_to_all x1, starting transfers between devices, from_everyone(): lax.all_to_all(jnp.broadcast_to(value[None], (size, *value.shape)), axis,...  7.71 us
  transfers between devices with their start and end apart: 1, of which 1 were waited for; matrix products, arithmetic and copies ran while one was open for 0% of the time, Pallas kernels for 0%

commit v1 on v0

v1 whole, which is shorter than its diff:
```python
import jax
import jax.numpy as jnp
from jax import lax
from jax.sharding import Mesh
from jax.sharding import PartitionSpec as P

PROW = ("prow_0", "prow_1")
PCOL = ("pcol_0", "pcol_1")
LINE = "pcol_0"
CORE = "pcol_1"


EPSILON = 1e-06


def product(left, right):
    return jnp.dot(left, right, precision=lax.Precision.HIGHEST)


def packed(value):
    rows = value.shape[0] // 2
    return jnp.concatenate([value[:rows], value[rows:]], axis=1)


def unpacked(value):
    lanes = value.shape[1] // 2
    return jnp.concatenate([value[:, :lanes], value[:, lanes:]], axis=0)


def from_everyone(value, axis):
    size = lax.axis_size(axis)
    return lax.all_to_all(
        jnp.broadcast_to(value[None], (size, *value.shape)), axis, 0, 0, tiled=True
    )


def over_copies(value, axis):
    return jnp.sum(from_everyone(value, axis), axis=0)


def shards(schur, panel_inverse, coupling, zslab, targets, pair_flags):
    block_size = schur.shape[2]
    row_blocks = schur.shape[0]
    window = coupling.shape[3]
    zrow_blocks = zslab.shape[0]
    half_blocks = row_blocks // 2
    panel_part = panel_inverse.shape[3] * block_size
    cores = lax.axis_size(CORE)
    line = lax.axis_size(LINE)
    share = targets.shape[0] // cores
    core = lax.axis_index(CORE)

    inverse = lax.all_gather(panel_inverse.reshape(2, block_size, panel_part), CORE, axis=1, tiled=True)
    strip = coupling.reshape(row_blocks * block_size, window)
    triangle = lax.all_gather(
        schur[:half_blocks, 0, :, 1, 0, :].reshape(half_blocks * block_size, block_size),
        CORE, axis=1, tiled=True,
    )
    z_rows = [
        lax.all_gather(
            zslab[:, 0, :, j, 0, :].reshape(zrow_blocks * block_size, block_size), CORE, axis=1, tiled=True
        )
        for j in range(2)
    ]

    own_targets = lax.dynamic_slice_in_dim(targets, core * share, share)
    own_flags = lax.dynamic_slice_in_dim(pair_flags, core * share, share)
    columns = jnp.arange(window, dtype=jnp.int32)[:, None]
    selection = (columns == own_targets[None, :]).astype(jnp.float32) + own_flags[None, :].astype(
        jnp.float32
    ) * (columns == own_targets[None, :] + 1).astype(jnp.float32)
    right_side = -product(strip, selection)
    early, late = right_side[:panel_part], right_side[panel_part:]

    later = unpacked(over_copies(packed(product(inverse[1], late)), PROW))
    partial_value = packed(product(triangle, later))
    pieces = lax.all_to_all(partial_value.reshape(line, -1, partial_value.shape[1]), LINE, 0, 0, tiled=True)
    summed = from_everyone(jnp.sum(pieces, axis=0), LINE).reshape(partial_value.shape)
    residual = early - unpacked(summed)
    sooner = unpacked(over_copies(packed(product(inverse[0], residual)), PROW))
    transformed = packed(product(z_rows[0], sooner) + product(z_rows[1], later))
    lanes = transformed.shape[1]
    stacked = jnp.moveaxis(
        transformed.reshape(zrow_blocks // 2, line, block_size // line, lanes), 1, 0
    )
    owned = jnp.sum(lax.all_to_all(stacked, LINE, 0, 0, tiled=True), axis=0)
    both = lax.all_gather(owned, CORE, axis=0, tiled=False)
    squares = jnp.sum(both * both, axis=(1, 2)).reshape(cores, 2, share).sum(axis=1).reshape(1, cores * share)
    squares = over_copies(over_copies(squares, LINE), PROW)
    total_rows = zrow_blocks * block_size * lax.axis_size(PROW)
    divisor = jnp.sqrt(squares / total_rows + EPSILON)
    rows = block_size // line // cores
    mine = lax.dynamic_slice_in_dim(both, core * rows, rows, axis=2)
    mine = mine.reshape(cores, zrow_blocks // 2, rows, 2, share).transpose(3, 1, 2, 0, 4)
    mine = mine.reshape(zrow_blocks, 1, rows, cores * share)
    return mine / divisor[None, None]


def solution(mesh):
    split = Mesh(mesh.devices.reshape(4, 4, 16, 2), ("prow_0", "prow_1", "pcol_0", "pcol_1"))
    placed = (
        P(None, PROW, None, None, PCOL, None),
        P(None, PCOL, None, None, PROW, None),
        P(None, PROW, None, None),
        P(None, PROW, None, None, PCOL, None),
        P(),
        P(),
    )
    return jax.shard_map(
        shards, mesh=split, in_specs=placed, out_specs=P(None, PROW, PCOL, None), check_vma=False
    )
```

time: 158 us -> 148 us (0.937)
  blocking collectives: 126 us -> 77.5 us
  waiting for transfers between devices: 14.6 us -> 38.3 us
  starting transfers between devices: 7.71 us -> 16.3 us
  local copies, waits for them, and re-layouts: 5.23 us -> 7.88 us
  other arithmetic: 1.63 us -> 3.39 us
    all_to_all x4 -> x1, blocking collectives: 63.2 us -> 14.3 us  [from_everyone(): lax.all_to_all(jnp.broadcast_to(value[None], (size, *value.shape)), axis,...]
    all_gather x0 -> x5, blocking collectives: none -> 24.2 us  [the longest x1 8.65 us: shards(): lax.all_gather(panel_inverse.reshape(2, block_size, panel_part), CORE, ax...]
    all_to_all x1 -> x4, waiting for transfers between devices: 14.6 us -> 38.3 us  [from_everyone(): lax.all_to_all(jnp.broadcast_to(value[None], (size, *value.shape)), axis,...]
    all_to_all x2, blocking collectives: 62.3 us -> 39 us  [the longest x1 23.6 us: shards(): lax.all_to_all(partial_value.reshape(line, -1, partial_value.shape[1]), L...]
    all_to_all x1 -> x4, starting transfers between devices: 7.71 us -> 16.3 us  [from_everyone(): lax.all_to_all(jnp.broadcast_to(value[None], (size, *value.shape)), axis,...]
    unnamed x0 -> x1, other arithmetic: none -> 2.36 us
    broadcast_in_dim x5 -> x6, local copies, waits for them, and re-layouts: 1.23 us -> 3.5 us  [from_everyone(): jnp.broadcast_to(value[None], (size, *value.shape))]
  transfers between devices with their start and end apart: 1 -> 4, of which waited for: 1 -> 4; matrix products, arithmetic and copies ran while one was open for 0% -> 1% of each run, Pallas kernels for 0% -> 0%
where the time goes in v1:
time: 148 us; the launch traced here: 147 us
  blocking collectives  77.5 us (52%)
  waiting for transfers between devices  38.3 us (26%)
  starting transfers between devices  16.3 us (11%)
  local copies, waits for them, and re-layouts  7.88 us (5%)
  other arithmetic  3.39 us (2%)
  matrix products  3.13 us (2%)
    all_to_all x4, waiting for transfers between devices, from_everyone(): lax.all_to_all(jnp.broadcast_to(value[None], (size, *value.shape)), axis,...  38.3 us
    all_to_all x1, blocking collectives, shards(): lax.all_to_all(partial_value.reshape(line, -1, partial_value.shape[1]), L...  23.6 us
    all_to_all x4, starting transfers between devices, from_everyone(): lax.all_to_all(jnp.broadcast_to(value[None], (size, *value.shape)), axis,...  16.3 us
    all_to_all x1, blocking collectives, shards(): owned = jnp.sum(lax.all_to_all(stacked, LINE, 0, 0, tiled=True), axis=0)  15.3 us
    all_to_all x1, blocking collectives, from_everyone(): lax.all_to_all(jnp.broadcast_to(value[None], (size, *value.shape)), axis,...  14.3 us
    all_gather x1, blocking collectives, shards(): lax.all_gather(panel_inverse.reshape(2, block_size, panel_part), CORE, ax...  8.65 us
    all_gather x2, blocking collectives, shards(): lax.all_gather(zslab[:, 0, :, j, 0, :].reshape(zrow_blocks * block_size,...  7.01 us
    all_gather x1, blocking collectives, shards(): both = lax.all_gather(owned, CORE, axis=0, tiled=False)  6.58 us
  transfers between devices with their start and end apart: 4, of which 4 were waited for; matrix products, arithmetic and copies ran while one was open for 1% of the time, Pallas kernels for 0%

profile of v1, /device:TPU:1, one launch (start us, length us, event | category | flops | bytes accessed | tf_op | source)
XLA Modules:
  0.0 146.7 jit_solution(9932559897815496460)
XLA Ops:
  0.0 0.7 copy-done.2
  0.8 0.6 copy-done.3
  1.4 0.5 broadcast.43
  2.0 2.4 %reduce.5 = f32[2,128,2,128]{3,2,1,0:T(2,128)S(1)} reduce(f32[2,1,128,2,1,128]{5,4,3,2,1,0:T(1,128)} %param.7, f32[]{:T(128)} %broadcast.43), dimensions={1,4}, to_apply=%param.7.reduce_sub_computation.3 | reduce | bytes 524292 | tf_op args[1]
  4.5 8.6 %all_gather.18 = f32[2,256,256]{2,1,0:T(8,128)S(1)} all-gather(f32[2,128,256]{2,1,0:T(8,128)S(1)} %reshape.66), channel_id=1, replica_groups=mesh['prow_0'=4,'prow_1'=4,'pcol_0'=16,'pcol_1'=2] {'pcol_1'}, dimensions={1}, use_global_device_ids=true | all-gather | bytes 786432 | tf_op jit(solution)/shard_map/all_gather | solution.py:53
  13.2 0.7 fusion.1
  14.3 1.1 broadcast_in_dim.12
  15.4 3.7 %all-to-all-start = ((f32[16,128,128]{2,1,0:T(8,128)}), f32[16,128,128]{2,1,0:T(8,128)S(1)}, u32[]{:S(2)}, u32[]{:S(2)}) async-start(f32[16,128,128]{2,1,0:T(8,128)} %broadcast_in_dim.12), calls=%async_computation | async-start | bytes 2097152 | tf_op jit(solution)/shard_map/all_to_all | solution.py:32
  19.1 0.9 slice.70
  20.0 2.0 %all_gather.19 = f32[256,256]{1,0:T(8,128)S(1)} all-gather(f32[256,128]{1,0:T(8,128)S(1)} %bitcast.39), channel_id=1, replica_groups=mesh['prow_0'=4,'prow_1'=4,'pcol_0'=16,'pcol_1'=2] {'pcol_1'}, dimensions={1}, use_global_device_ids=true | all-gather | bytes 393216 | tf_op jit(solution)/shard_map/all_gather | solution.py:55
  22.0 13.9 %all-to-all-done = f32[16,128,128]{2,1,0:T(8,128)S(1)} async-done(((f32[16,128,128]{2,1,0:T(8,128)}), f32[16,128,128]{2,1,0:T(8,128)S(1)}, u32[]{:S(2)}, u32[]{:S(2)}) %all-to-all-start) | async-done | bytes 1048608 | tf_op jit(solution)/shard_map/all_to_all | solution.py:32
  36.1 0.4 convolution_bitcast_fusion.2
  36.6 23.6 %all_to_all.35 = f32[16,8,128]{2,1,0:T(8,128)S(1)} all-to-all(f32[16,8,128]{2,1,0:T(8,128)S(1)} %bitcast.41), channel_id=1, replica_groups=mesh['prow_0'=4,'prow_1'=4,'pcol_0'=16,'pcol_1'=2] {'pcol_0'}, dimensions={0} | all-to-all | bytes 131072 | tf_op jit(solution)/shard_map/all_to_all | solution.py:77
  60.3 14.3 %all_to_all.36 = f32[16,8,128]{2,1,0:T(8,128)S(1)} all-to-all(f32[16,8,128]{2,1,0:T(8,128)S(1)} %broadcast_in_dim.13), channel_id=1, replica_groups=mesh['prow_0'=4,'prow_1'=4,'pcol_0'=16,'pcol_1'=2] {'pcol_0'}, dimensions={0} | all-to-all | bytes 131072 | tf_op jit(solution)/shard_map/all_to_all | solution.py:32
  74.8 0.4 convolution_bitcast_fusion
  75.3 1.1 broadcast_in_dim.14
  76.4 5.6 %all-to-all-start.3 = ((f32[16,128,128]{2,1,0:T(8,128)}), f32[16,128,128]{2,1,0:T(8,128)S(1)}, u32[]{:S(2)}, u32[]{:S(2)}) async-start(f32[16,128,128]{2,1,0:T(8,128)} %broadcast_in_dim.14), calls=%async_computation.3 | async-start | bytes 2097152 | tf_op jit(solution)/shard_map/all_to_all | solution.py:32
  82.0 0.4 fusion.22
  82.4 4.8 %all_gather.20 = f32[512,256]{1,0:T(8,128)S(1)} all-gather(f32[512,128]{1,0:T(8,128)S(1)} %bitcast.37), channel_id=1, replica_groups=mesh['prow_0'=4,'prow_1'=4,'pcol_0'=16,'pcol_1'=2] {'pcol_1'}, dimensions={1}, use_global_device_ids=true | all-gather | bytes 786432 | tf_op jit(solution)/shard_map/all_gather | solution.py:60
  87.3 2.2 %all_gather.21 = f32[512,256]{1,0:T(8,128)S(1)} all-gather(f32[512,128]{1,0:T(8,128)S(1)} %bitcast.36), channel_id=1, replica_groups=mesh['prow_0'=4,'prow_1'=4,'pcol_0'=16,'pcol_1'=2] {'pcol_1'}, dimensions={1}, use_global_device_ids=true | all-gather | bytes 786432 | tf_op jit(solution)/shard_map/all_gather | solution.py:60
  89.4 7.0 %all-to-all-done.3 = f32[16,128,128]{2,1,0:T(8,128)S(1)} async-done(((f32[16,128,128]{2,1,0:T(8,128)}), f32[16,128,128]{2,1,0:T(8,128)S(1)}, u32[]{:S(2)}, u32[]{:S(2)}) %all-to-all-start.3) | async-done | bytes 1048608 | tf_op jit(solution)/shard_map/all_to_all | solution.py:32
  96.6 0.7 fusion.2
  97.3 0.7 fusion
  98.1 15.3 %all_to_all.37 = f32[16,2,8,128]{3,2,1,0:T(8,128)S(1)} all-to-all(f32[16,2,8,128]{3,2,1,0:T(8,128)S(1)} %copy.47), channel_id=1, replica_groups=mesh['prow_0'=4,'prow_1'=4,'pcol_0'=16,'pcol_1'=2] {'pcol_0'}, dimensions={0} | all-to-all | bytes 262144 | tf_op jit(solution)/shard_map/all_to_all | solution.py:86
  113.4 6.6 %all-gather = f32[4,8,128]{2,1,0:T(8,128)S(1)} all-gather(f32[2,8,128]{2,1,0:T(8,128)S(1)} %reduce_sum.75), channel_id=2, replica_groups=mesh['prow_0'=4,'prow_1'=4,'pcol_0'=16,'pcol_1'=2] {'pcol_1'}, dimensions={0}, use_global_device_ids=true | all-gather | bytes 24576 | tf_op jit(solution)/shard_map/all_gather | solution.py:87
  120.2 0.6 broadcast_in_dim.16
  120.8 3.6 %all-to-all-start.5 = ((f32[16,1,128]{2,1,0:T(1,128)}), f32[16,1,128]{2,1,0:T(1,128)S(1)}, u32[]{:S(2)}, u32[]{:S(2)}) async-start(f32[16,1,128]{2,1,0:T(1,128)} %broadcast_in_dim.16), calls=%async_computation.5 | async-start | bytes 16384 | tf_op jit(solution)/shard_map/all_to_all | solution.py:32
  124.4 11.3 %all-to-all-done.5 = f32[16,1,128]{2,1,0:T(1,128)S(1)} async-done(((f32[16,1,128]{2,1,0:T(1,128)}), f32[16,1,128]{2,1,0:T(1,128)S(1)}, u32[]{:S(2)}, u32[]{:S(2)}) %all-to-all-start.5) | async-done | bytes 8224 | tf_op jit(solution)/shard_map/all_to_all | solution.py:32
  135.7 0.6 broadcast_in_dim.17
  136.3 3.5 %all-to-all-start.6 = ((f32[16,1,128]{2,1,0:T(1,128)}), f32[16,1,128]{2,1,0:T(1,128)S(1)}, u32[]{:S(2)}, u32[]{:S(2)}) async-start(f32[16,1,128]{2,1,0:T(1,128)} %broadcast_in_dim.17), calls=%async_computation.6 | async-start | bytes 16384 | tf_op jit(solution)/shard_map/all_to_all | solution.py:32
  140.0 6.1 %all-to-all-done.6 = f32[16,1,128]{2,1,0:T(1,128)S(1)} async-done(((f32[16,1,128]{2,1,0:T(1,128)}), f32[16,1,128]{2,1,0:T(1,128)S(1)}, u32[]{:S(2)}, u32[]{:S(2)}) %all-to-all-start.6) | async-done | bytes 8224 | tf_op jit(solution)/shard_map/all_to_all | solution.py:32
  146.1 0.6 divide_bitcast_fusion
  (44 shorter events, 2.2 us)
Async XLA Ops:
  0.0 13.2 %copy-start = (f32[4,1,128,256]{3,2,1,0:T(8,128)S(1)}, f32[4,1,128,256]{3,2,1,0:T(8,128)}, u32[]{:S(2)}) copy-start(f32[4,1,128,256]{3,2,1,0:T(8,128)} %param.8) | copy-start | bytes 1572868
  0.0 0.7 copy-start.2
  0.7 0.7 copy-start.3
  15.4 20.5 %all-to-all-start = ((f32[16,128,128]{2,1,0:T(8,128)}), f32[16,128,128]{2,1,0:T(8,128)S(1)}, u32[]{:S(2)}, u32[]{:S(2)}) async-start(f32[16,128,128]{2,1,0:T(8,128)} %broadcast_in_dim.12), calls=%async_computation | async-start | bytes 2097152 | tf_op jit(solution)/shard_map/all_to_all | solution.py:32
  76.4 5.6 %copy-start.1 = (f32[4,1,128,2,1,128]{5,4,3,2,1,0:T(1,128)S(1)}, f32[4,1,128,2,1,128]{5,4,3,2,1,0:T(1,128)}, u32[]{:S(2)}) copy-start(f32[4,1,128,2,1,128]{5,4,3,2,1,0:T(1,128)} %param.9) | copy-start | bytes 1572868
  76.4 20.0 %all-to-all-start.3 = ((f32[16,128,128]{2,1,0:T(8,128)}), f32[16,128,128]{2,1,0:T(8,128)S(1)}, u32[]{:S(2)}, u32[]{:S(2)}) async-start(f32[16,128,128]{2,1,0:T(8,128)} %broadcast_in_dim.14), calls=%async_computation.3 | async-start | bytes 2097152 | tf_op jit(solution)/shard_map/all_to_all | solution.py:32
  120.8 14.8 %all-to-all-start.5 = ((f32[16,1,128]{2,1,0:T(1,128)}), f32[16,1,128]{2,1,0:T(1,128)S(1)}, u32[]{:S(2)}, u32[]{:S(2)}) async-start(f32[16,1,128]{2,1,0:T(1,128)} %broadcast_in_dim.16), calls=%async_computation.5 | async-start | bytes 16384 | tf_op jit(solution)/shard_map/all_to_all | solution.py:32
  136.3 9.8 %all-to-all-start.6 = ((f32[16,1,128]{2,1,0:T(1,128)}), f32[16,1,128]{2,1,0:T(1,128)S(1)}, u32[]{:S(2)}, u32[]{:S(2)}) async-start(f32[16,1,128]{2,1,0:T(1,128)} %broadcast_in_dim.17), calls=%async_computation.6 | async-start | bytes 16384 | tf_op jit(solution)/shard_map/all_to_all | solution.py:32

commit v2 on v1

v2 whole, which is shorter than its diff:
```python
import functools

import jax
import jax.numpy as jnp
from jax import lax
from jax.experimental import pallas as pl
from jax.experimental.pallas import tpu as pltpu
from jax.sharding import Mesh
from jax.sharding import PartitionSpec as P

PROW = ("prow_0", "prow_1")
PCOL = ("pcol_0", "pcol_1")
LINE = "pcol_0"
CORE = "pcol_1"


EPSILON = 1e-06


def product(left, right):
    return jnp.dot(left, right, precision=lax.Precision.HIGHEST, preferred_element_type=jnp.float32)


def exchanged(value, axis):
    return lax.all_to_all(value, axis, 0, 0, tiled=True)


def first_half(shape):
    return lax.broadcasted_iota(jnp.int32, shape, 1) < shape[1] // 2


def turned(value):
    return pltpu.roll(value, value.shape[1] // 2, 1)


def doubled(value):
    left, other = first_half(value.shape), turned(value)
    return jnp.where(left, value, other), jnp.where(left, other, value)


def merged(low, high):
    return jnp.where(first_half(low.shape), low, high)


def strided(ref, core, start, count, step):
    return ref[core, pl.ds(start, count, stride=step), :]


def begin(core_ref, targets_ref, flags_ref, strip_ref, inverse_ref, sent_ref, early_ref, *, block):
    window = strip_ref.shape[1]
    panel = strip_ref.shape[0] // 2
    parts = panel // block
    lanes = targets_ref.shape[1]
    home = first_half((1, lanes)) == (core_ref[0] == 0)
    targets = jnp.where(home, targets_ref[...], turned(targets_ref[...]))
    flags = jnp.where(home, flags_ref[...], turned(flags_ref[...])).astype(jnp.float32)
    columns = lax.broadcasted_iota(jnp.int32, (window, lanes), 0)
    selection = (columns == targets).astype(jnp.float32) + flags * (columns == targets + 1).astype(
        jnp.float32
    )
    late = -product(strip_ref[panel:, :], selection)
    applied = []
    for core in range(2):
        applied.append(
            sum(
                product(
                    strided(inverse_ref, core, parts * block + part, block, parts),
                    late[part * block : (part + 1) * block],
                )
                for part in range(parts)
            )
        )
    out = merged(*applied)
    for peer in range(sent_ref.shape[0]):
        sent_ref[peer] = out
    early_ref[...] = -product(strip_ref[:panel, :], selection)


def coupled(pieces_ref, triangle_ref, sent_ref, later_ref, *, block):
    later = jnp.sum(pieces_ref[...], axis=0)
    later_ref[...] = later
    halves = doubled(later)
    values = []
    for part in range(2):
        values.append(
            sum(
                product(strided(triangle_ref, core, part * 2 * block + 1, block, 2), halves[core])
                for core in range(2)
            )
        )
    sent_ref[...] = merged(*values)


def solved(summed_ref, early_ref, inverse_ref, sent_ref, *, block):
    halves = doubled(summed_ref[...])
    parts = early_ref.shape[0] // block
    residual = [early_ref[part * block : (part + 1) * block, :] - halves[part] for part in range(parts)]
    applied = []
    for core in range(2):
        applied.append(
            sum(
                product(strided(inverse_ref, core, part, block, parts), residual[part])
                for part in range(parts)
            )
        )
    out = merged(*applied)
    for peer in range(sent_ref.shape[0]):
        sent_ref[peer] = out


def carried(pieces_ref, later_ref, low_ref, high_ref, sent_ref, *, block):
    sooner = doubled(jnp.sum(pieces_ref[...], axis=0))
    later = doubled(later_ref[...])
    values = []
    for ref in (low_ref, high_ref):
        rows = ref.shape[1] // 2
        values.append(
            sum(
                product(strided(ref, core, 0, rows, 2), sooner[core])
                + product(strided(ref, core, 1, rows, 2), later[core])
                for core in range(2)
            )
        )
    out = merged(*values)
    peers, stacks, rows, lanes = sent_ref.shape
    for stack in range(stacks):
        sent_ref[:, stack] = out[stack * block : (stack + 1) * block].reshape(peers, rows, lanes)


def squared(both_ref, sent_ref):
    both = both_ref[...]
    cores, stacks, rows, lanes = both.shape
    squares = jnp.sum((both * both).reshape(cores, stacks * rows, lanes), axis=1)
    squares = squares + turned(squares)
    out = merged(squares[0:1], squares[1:2])
    sent_ref[...] = jnp.broadcast_to(out[None], sent_ref.shape)


def again(pieces_ref, sent_ref):
    sent_ref[...] = jnp.broadcast_to(jnp.sum(pieces_ref[...], axis=0, keepdims=True), sent_ref.shape)


def finished(core_ref, both_ref, pieces_ref, out_ref, *, total):
    squares = jnp.sum(pieces_ref[...], axis=0)
    divisor = jnp.sqrt(squares / total + EPSILON)
    stacks = both_ref.shape[1]
    rows = out_ref.shape[2]
    for stack in range(stacks):
        low = both_ref[0, stack]
        high = both_ref[1, stack]
        for side, value in enumerate((merged(low, turned(high)), merged(turned(low), high))):
            value = value / divisor
            own = jnp.where(core_ref[0] == 0, value[:rows], value[rows:])
            out_ref[side * stacks + stack, 0] = own


LIMIT = 12 * 2**20
SCALAR = pl.BlockSpec(memory_space=pltpu.SMEM)
LOCAL = pl.BlockSpec(memory_space=pltpu.VMEM)


def kernel(body, shapes, *args, scalars=0, **settings):
    outs = [jax.ShapeDtypeStruct(shape, jnp.float32) for shape in shapes]
    single = len(outs) == 1
    return pl.pallas_call(
        functools.partial(body, **settings),
        out_shape=outs[0] if single else outs,
        in_specs=[SCALAR] * scalars + [LOCAL] * (len(args) - scalars),
        out_specs=LOCAL if single else [LOCAL] * len(outs),
        name=body.__name__,
        compiler_params=pltpu.CompilerParams(vmem_limit_bytes=LIMIT),
    )(*args)


def shards(schur, panel_inverse, coupling, zslab, targets, pair_flags):
    block = schur.shape[2]
    row_blocks = schur.shape[0]
    window = coupling.shape[3]
    zrow_blocks = zslab.shape[0]
    count = targets.shape[0]
    line = lax.axis_size(LINE)
    peers = lax.axis_size(PROW)
    panel = panel_inverse.shape[3] * block
    core = lax.axis_index(CORE).astype(jnp.int32).reshape(1)

    inverse = lax.all_gather(panel_inverse.reshape(-1, block), CORE)
    strip = coupling.reshape(row_blocks * block, window)
    sent, early = kernel(
        begin,
        [(peers, block, count), (panel, count)],
        core, targets.reshape(1, count), pair_flags.reshape(1, count), strip, inverse,
        scalars=1, block=block,
    )
    pieces = exchanged(sent, PROW)
    triangle = lax.all_gather(schur[: row_blocks // 2].reshape(-1, block), CORE)
    low = lax.all_gather(zslab[: zrow_blocks // 2].reshape(-1, block), CORE)
    high = lax.all_gather(zslab[zrow_blocks // 2 :].reshape(-1, block), CORE)
    pieces, triangle, low, high = lax.optimization_barrier((pieces, triangle, low, high))
    partial_value, later = kernel(
        coupled, [(block, count), (block, count)], pieces, triangle, block=block
    )
    parts = exchanged(partial_value.reshape(line, -1, count), LINE)
    mine = jnp.sum(parts, axis=0)
    summed = exchanged(jnp.broadcast_to(mine[None], (line, *mine.shape)), LINE).reshape(block, count)
    sent = kernel(solved, [(peers, block, count)], summed, early, inverse, block=block)
    pieces = exchanged(sent, PROW)
    stacked = kernel(
        carried,
        [(line, zrow_blocks // 2, block // line, count)],
        pieces, later, low, high, block=block,
    )
    owned = jnp.sum(exchanged(stacked, LINE), axis=0)
    both = lax.all_gather(owned, CORE)
    squares = exchanged(kernel(squared, [(line, 1, count)], both), LINE)
    squares = exchanged(kernel(again, [(peers, 1, count)], squares), PROW)
    total = zrow_blocks * block * peers
    rows = block // line // lax.axis_size(CORE)
    return kernel(
        finished, [(zrow_blocks, 1, rows, count)], core, both, squares, scalars=1, total=total
    )


def solution(mesh):
    split = Mesh(mesh.devices.reshape(4, 4, 16, 2), ("prow_0", "prow_1", "pcol_0", "pcol_1"))
    placed = (
        P(None, PROW, None, None, PCOL, None),
        P(None, PCOL, None, None, PROW, None),
        P(None, PROW, None, None),
        P(None, PROW, None, None, PCOL, None),
        P(),
        P(),
    )
    return jax.shard_map(
        shards, mesh=split, in_specs=placed, out_specs=P(None, PROW, PCOL, None), check_vma=False
    )
```

time: 148 us -> 140 us (0.946)
  blocking collectives: 77.5 us -> 119 us
  waiting for transfers between devices: 38.3 us -> 8.79 us
  starting transfers between devices: 16.3 us -> 3.65 us
  local copies, waits for them, and re-layouts: 7.88 us -> 2.08 us
  Pallas kernels: 0 us -> 4.88 us
  other arithmetic: 3.39 us -> 0.04 us
  matrix products: 3.13 us -> 0 us
    all_to_all x3 -> x6, blocking collectives: 53.3 us -> 97.2 us  [exchanged(): return lax.all_to_all(value, axis, 0, 0, tiled=True)]
    all_to_all x4 -> x1, waiting for transfers between devices: 38.3 us -> 8.79 us  [exchanged(): return lax.all_to_all(value, axis, 0, 0, tiled=True)]
    all_to_all x4 -> x1, starting transfers between devices: 16.3 us -> 3.65 us  [exchanged(): return lax.all_to_all(value, axis, 0, 0, tiled=True)]
    pallas_call x0 -> x7, Pallas kernels: none -> 4.88 us  [kernel(): pl.pallas_call(functools.partial(body, **settings), out_shape=outs[0] if...]
    broadcast_in_dim x6 -> x1, local copies, waits for them, and re-layouts: 3.5 us -> 0.01 us  [shards(): jnp.broadcast_to(mine[None], (line, *mine.shape))]
    dot_general x6 -> x0, matrix products: 3.13 us -> none  [product(): return jnp.dot(left, right, precision=lax.Precision.HIGHEST)]
    all_gather x5, blocking collectives: 24.2 us -> 21.6 us  [the longest x1 8.98 us: shards(): inverse = lax.all_gather(panel_inverse.reshape(-1, block), CORE)]
    unnamed x1 -> x0, other arithmetic: 2.36 us -> none
  transfers between devices with their start and end apart: 4 -> 1, of which waited for: 4 -> 1; matrix products, arithmetic and copies ran while one was open for 1% -> 0% of each run, Pallas kernels for 0% -> 0%
where the time goes in v2:
time: 140 us; the launch traced here: 138 us
  blocking collectives  119 us (85%)
  waiting for transfers between devices  8.79 us (6%)
  Pallas kernels  4.88 us (3%)
  starting transfers between devices  3.65 us (3%)
  local copies, waits for them, and re-layouts  2.08 us (1%)
    all_to_all x6, blocking collectives, exchanged(): return lax.all_to_all(value, axis, 0, 0, tiled=True)  97.2 us
    all_gather x1, blocking collectives, shards(): inverse = lax.all_gather(panel_inverse.reshape(-1, block), CORE)  8.98 us
    all_to_all x1, waiting for transfers between devices, exchanged(): return lax.all_to_all(value, axis, 0, 0, tiled=True)  8.79 us
    all_gather x1, blocking collectives, shards(): both = lax.all_gather(owned, CORE)  5.95 us
    pallas_call x7, Pallas kernels, kernel(): pl.pallas_call(functools.partial(body, **settings), out_shape=outs[0] if...  4.88 us
    all_to_all x1, starting transfers between devices, exchanged(): return lax.all_to_all(value, axis, 0, 0, tiled=True)  3.65 us
  transfers between devices with their start and end apart: 1, of which 1 were waited for; matrix products, arithmetic and copies ran while one was open for 0% of the time, Pallas kernels for 0%

profile of v2, /device:TPU:1, one launch (start us, length us, event | category | flops | bytes accessed | tf_op | source)
XLA Modules:
  0.0 138.3 jit_solution(3546740124285417284)
XLA Ops:
  0.0 0.0 copy-start
  0.0 9.0 %all_gather.18.inverse_ref = f32[2,512,128]{2,1,0:T(8,128)S(1)} all-gather(f32[1,512,128]{2,1,0:T(8,128)} %bitcast.21), channel_id=1, replica_groups=mesh['prow_0'=4,'prow_1'=4,'pcol_0'=16,'pcol_1'=2] {'pcol_1'}, dimensions={0}, use_global_device_ids=true | all-gather | bytes 786432 | tf_op jit(solution)/shard_map/all_gather | solution.py:186
  9.0 0.0 copy-start.1
  9.0 0.0 copy-start.2
  9.0 0.0 copy-done
  9.0 0.6 copy-done.1
  9.6 0.0 copy-done.2
  9.7 2.0 %begin.1 = (f32[16,128,128]{2,1,0:T(8,128)}, f32[256,128]{1,0:T(8,128)S(1)}) custom-call(s32[1]{0:T(128)} %bitcast.core_ref, s32[1,128]{1,0:T(1,128)S(1)} %bitcast.16, s32[1,128]{1,0:T(1,128)S(1)} %bitcast.17, f32[512,256]{1,0:T(8,128)S(1)} %bitcast.11, f32[2,512,128]{2,1,0:T(8,128)S(1)} %all_gather.18.inverse_ref), custom_call_target="tpu_custom_call" | custom-call | tf_op jit(solution)/shard_map/begin/pallas_call | solution.py:165
  11.7 3.7 %all-to-all-start = ((f32[16,128,128]{2,1,0:T(8,128)}), f32[16,128,128]{2,1,0:T(8,128)S(1)}, u32[]{:S(2)}, u32[]{:S(2)}) async-start(f32[16,128,128]{2,1,0:T(8,128)} %get-tuple-element.13), calls=%async_computation | async-start | bytes 2097152 | tf_op jit(solution)/shard_map/all_to_all | solution.py:25
  15.4 0.0 copy-start.3
  15.4 1.0 copy-done.3
  16.4 0.4 fusion
  16.8 2.2 %all_gather.20.low_ref = f32[2,512,128]{2,1,0:T(8,128)S(1)} all-gather(f32[1,512,128]{2,1,0:T(8,128)S(1)} %bitcast.20), channel_id=1, replica_groups=mesh['prow_0'=4,'prow_1'=4,'pcol_0'=16,'pcol_1'=2] {'pcol_1'}, dimensions={0}, use_global_device_ids=true | all-gather | bytes 786432 | tf_op jit(solution)/shard_map/all_gather | solution.py:196
  18.9 0.0 slice-start
  18.9 2.3 %all_gather.21.high_ref = f32[2,512,128]{2,1,0:T(8,128)S(1)} all-gather(f32[1,512,128]{2,1,0:T(8,128)S(1)} %bitcast.19), channel_id=1, replica_groups=mesh['prow_0'=4,'prow_1'=4,'pcol_0'=16,'pcol_1'=2] {'pcol_1'}, dimensions={0}, use_global_device_ids=true | all-gather | bytes 786432 | tf_op jit(solution)/shard_map/all_gather | solution.py:197
  21.2 0.0 slice-done
  21.2 2.2 %all_gather.19.triangle_ref = f32[2,512,128]{2,1,0:T(8,128)S(1)} all-gather(f32[1,512,128]{2,1,0:T(8,128)S(1)} %bitcast.18), channel_id=1, replica_groups=mesh['prow_0'=4,'prow_1'=4,'pcol_0'=16,'pcol_1'=2] {'pcol_1'}, dimensions={0}, use_global_device_ids=true | all-gather | bytes 786432 | tf_op jit(solution)/shard_map/all_gather | solution.py:195
  23.4 8.8 %all-to-all-done.pieces_ref = f32[16,128,128]{2,1,0:T(8,128)S(1)} async-done(((f32[16,128,128]{2,1,0:T(8,128)}), f32[16,128,128]{2,1,0:T(8,128)S(1)}, u32[]{:S(2)}, u32[]{:S(2)}) %all-to-all-start) | async-done | bytes 1048608 | tf_op jit(solution)/shard_map/all_to_all | solution.py:25
  32.2 0.5 coupled.1
  32.7 23.6 %all_to_all.35 = f32[16,8,128]{2,1,0:T(8,128)S(1)} all-to-all(f32[16,8,128]{2,1,0:T(8,128)S(1)} %bitcast.15), channel_id=1, replica_groups=mesh['prow_0'=4,'prow_1'=4,'pcol_0'=16,'pcol_1'=2] {'pcol_0'}, dimensions={0} | all-to-all | bytes 131072 | tf_op jit(solution)/shard_map/all_to_all | solution.py:25
  56.3 14.3 %all_to_all.36 = f32[16,8,128]{2,1,0:T(8,128)S(1)} all-to-all(f32[16,8,128]{2,1,0:T(8,128)S(1)} %broadcast_in_dim.2), channel_id=1, replica_groups=mesh['prow_0'=4,'prow_1'=4,'pcol_0'=16,'pcol_1'=2] {'pcol_0'}, dimensions={0} | all-to-all | bytes 131072 | tf_op jit(solution)/shard_map/all_to_all | solution.py:25
  70.7 0.5 solved.1
  71.2 20.3 %all_to_all.37.pieces_ref = f32[16,128,128]{2,1,0:T(8,128)S(1)} all-to-all(f32[16,128,128]{2,1,0:T(8,128)S(1)} %solved.1), channel_id=1, replica_groups=mesh['prow_0'=4,'prow_1'=4,'pcol_0'=16,'pcol_1'=2] {'prow_0','prow_1'}, dimensions={0} | all-to-all | bytes 2097152 | tf_op jit(solution)/shard_map/all_to_all | solution.py:25
  91.5 1.1 carried.1
  92.6 15.3 %all_to_all.38 = f32[16,2,8,128]{3,2,1,0:T(8,128)S(1)} all-to-all(f32[16,2,8,128]{3,2,1,0:T(8,128)S(1)} %carried.1), channel_id=1, replica_groups=mesh['prow_0'=4,'prow_1'=4,'pcol_0'=16,'pcol_1'=2] {'pcol_0'}, dimensions={0} | all-to-all | bytes 262144 | tf_op jit(solution)/shard_map/all_to_all | solution.py:25
  107.9 6.0 %all-gather = f32[4,8,128]{2,1,0:T(8,128)S(1)} all-gather(f32[2,8,128]{2,1,0:T(8,128)S(1)} %reduce_sum.19), channel_id=2, replica_groups=mesh['prow_0'=4,'prow_1'=4,'pcol_0'=16,'pcol_1'=2] {'pcol_1'}, dimensions={0}, use_global_device_ids=true | all-gather | bytes 24576 | tf_op jit(solution)/shard_map/all_gather | solution.py:213
  113.8 0.1 squared.1
  113.9 14.7 %all_to_all.39.pieces_ref = f32[16,1,128]{2,1,0:T(1,128)S(1)} all-to-all(f32[16,1,128]{2,1,0:T(1,128)S(1)} %squared.1), channel_id=1, replica_groups=mesh['prow_0'=4,'prow_1'=4,'pcol_0'=16,'pcol_1'=2] {'pcol_0'}, dimensions={0} | all-to-all | bytes 16384 | tf_op jit(solution)/shard_map/all_to_all | solution.py:25
  128.7 9.0 %all_to_all.40.pieces_ref = f32[16,1,128]{2,1,0:T(1,128)S(1)} all-to-all(f32[16,1,128]{2,1,0:T(1,128)S(1)} %again.1), channel_id=1, replica_groups=mesh['prow_0'=4,'prow_1'=4,'pcol_0'=16,'pcol_1'=2] {'prow_0','prow_1'}, dimensions={0} | all-to-all | bytes 16384 | tf_op jit(solution)/shard_map/all_to_all | solution.py:25
  137.6 0.7 finished.1
  (4 shorter events, 0.1 us)
Async XLA Ops:
  0.0 9.0 %copy-start = (f32[4,1,128,256]{3,2,1,0:T(8,128)S(1)}, f32[4,1,128,256]{3,2,1,0:T(8,128)}, u32[]{:S(2)}) copy-start(f32[4,1,128,256]{3,2,1,0:T(8,128)} %param.8) | copy-start | bytes 1572868
  9.0 0.7 copy-start.1
  9.0 0.7 copy-start.2
  11.7 20.5 %all-to-all-start = ((f32[16,128,128]{2,1,0:T(8,128)}), f32[16,128,128]{2,1,0:T(8,128)S(1)}, u32[]{:S(2)}, u32[]{:S(2)}) async-start(f32[16,128,128]{2,1,0:T(8,128)} %get-tuple-element.13), calls=%async_computation | async-start | bytes 2097152 | tf_op jit(solution)/shard_map/all_to_all | solution.py:25
  15.4 1.0 copy-start.3
  18.9 2.3 %slice-start = ((f32[4,1,128,2,1,128]{5,4,3,2,1,0:T(1,128)}), f32[2,1,128,2,1,128]{5,4,3,2,1,0:T(1,128)S(1)}, s32[]{:S(2)}) async-start(f32[4,1,128,2,1,128]{5,4,3,2,1,0:T(1,128)} %param.6), calls=%async_computation.7 | async-start | bytes 524288 | tf_op jit(solution)/shard_map/slice | solution.py:195

commit v3 on v2

--- a/solution.py
+++ b/solution.py
@@ -46,64 +46,86 @@
     return ref[core, pl.ds(start, count, stride=step), :]
 
 
-def begin(core_ref, targets_ref, flags_ref, strip_ref, inverse_ref, sent_ref, early_ref, *, block):
-    window = strip_ref.shape[1]
-    panel = strip_ref.shape[0] // 2
-    parts = panel // block
+def selected(targets_ref, flags_ref, window):
     lanes = targets_ref.shape[1]
-    home = first_half((1, lanes)) == (core_ref[0] == 0)
-    targets = jnp.where(home, targets_ref[...], turned(targets_ref[...]))
-    flags = jnp.where(home, flags_ref[...], turned(flags_ref[...])).astype(jnp.float32)
+    targets = targets_ref[...]
     columns = lax.broadcasted_iota(jnp.int32, (window, lanes), 0)
-    selection = (columns == targets).astype(jnp.float32) + flags * (columns == targets + 1).astype(
+    flags = flags_ref[...].astype(jnp.float32)
+    chosen = (columns == targets).astype(jnp.float32) + flags * (columns == targets + 1).astype(
         jnp.float32
     )
-    late = -product(strip_ref[panel:, :], selection)
-    applied = []
-    for core in range(2):
-        applied.append(
-            sum(
-                product(
-                    strided(inverse_ref, core, parts * block + part, block, parts),
-                    late[part * block : (part + 1) * block],
-                )
-                for part in range(parts)
-            )
-        )
-    out = merged(*applied)
+    return chosen.astype(jnp.bfloat16)
+
+
+def thirds(value):
+    high = value.astype(jnp.bfloat16)
+    rest = value - high.astype(jnp.float32)
+    middle = rest.astype(jnp.bfloat16)
+    low = (rest - middle.astype(jnp.float32)).astype(jnp.bfloat16)
+    return high, middle, low
+
+
+def picked(parts, chosen):
+    return sum(jnp.dot(part, chosen, preferred_element_type=jnp.float32) for part in reversed(parts))
+
+
+def across(value, core):
+    left, right = doubled(value)
+    return jnp.where(core == 0, left, right)
+
+
+def begin(
+    strip_hbm, targets_hbm, flags_hbm, inverse_hbm,
+    sent_ref, strip_ref, targets_ref, flags_ref, inverse_ref, sems,
+):
+    panel, window = strip_ref.shape
+    block = sent_ref.shape[1]
+    half = inverse_ref.shape[1]
+    copies = [
+        pltpu.make_async_copy(strip_hbm.at[pl.ds(panel, panel)], strip_ref, sems.at[0]),
+        pltpu.make_async_copy(targets_hbm, targets_ref, sems.at[1]),
+        pltpu.make_async_copy(flags_hbm, flags_ref, sems.at[2]),
+        pltpu.make_async_copy(inverse_hbm.at[pl.ds(half, half)], inverse_ref.at[0], sems.at[3]),
+    ]
+    for copy in copies:
+        copy.start()
+    copies[1].wait()
+    copies[2].wait()
+    chosen = selected(targets_ref, flags_ref, window)
+    copies[0].wait()
+    late = -picked(thirds(strip_ref[...]), chosen)
+    copies[3].wait()
+    out = product(columns_of(inverse_ref, 0, 0, block), late)
     for peer in range(sent_ref.shape[0]):
         sent_ref[peer] = out
-    early_ref[...] = -product(strip_ref[:panel, :], selection)
-
-
-def coupled(pieces_ref, triangle_ref, sent_ref, later_ref, *, block):
-    later = jnp.sum(pieces_ref[...], axis=0)
-    later_ref[...] = later
-    halves = doubled(later)
+
+
+def columns_of(ref, core, start, count):
+    return jnp.concatenate(
+        [strided(ref, core, start, count, 2), strided(ref, core, start + 1, count, 2)], axis=1
+    )
+
+
+def opening(core_ref, targets_ref, flags_ref, strip_ref, early_ref):
+    panel = strip_ref.shape[0] // 2
+    chosen = selected(targets_ref, flags_ref, strip_ref.shape[1])
+    early_ref[...] = across(-picked(thirds(strip_ref[:panel, :]), chosen), core_ref[0])
+
+
+def coupled(core_ref, solved_ref, triangle_ref, sent_ref, later_ref, *, block):
+    halves = [across(solved_ref[core], core_ref[0]) for core in range(2)]
+    later_ref[...] = merged(*halves)
+    both = jnp.concatenate(halves, axis=0)
     values = []
     for part in range(2):
-        values.append(
-            sum(
-                product(strided(triangle_ref, core, part * 2 * block + 1, block, 2), halves[core])
-                for core in range(2)
-            )
-        )
+        blocks = [strided(triangle_ref, core, part * 2 * block + 1, block, 2) for core in range(2)]
+        values.append(product(jnp.concatenate(blocks, axis=1), both))
     sent_ref[...] = merged(*values)
 
 
 def solved(summed_ref, early_ref, inverse_ref, sent_ref, *, block):
-    halves = doubled(summed_ref[...])
-    parts = early_ref.shape[0] // block
-    residual = [early_ref[part * block : (part + 1) * block, :] - halves[part] for part in range(parts)]
-    applied = []
-    for core in range(2):
-        applied.append(
-            sum(
-                product(strided(inverse_ref, core, part, block, parts), residual[part])
-                for part in range(parts)
-            )
-        )
-    out = merged(*applied)
+    residual = early_ref[...] - jnp.concatenate(doubled(summed_ref[...]), axis=0)
+    out = merged(*[product(columns_of(inverse_ref, core, 0, block), residual) for core in range(2)])
     for peer in range(sent_ref.shape[0]):
         sent_ref[peer] = out
 
@@ -111,16 +133,11 @@
 def carried(pieces_ref, later_ref, low_ref, high_ref, sent_ref, *, block):
     sooner = doubled(jnp.sum(pieces_ref[...], axis=0))
     later = doubled(later_ref[...])
+    known = [jnp.concatenate([sooner[core], later[core]], axis=0) for core in range(2)]
     values = []
     for ref in (low_ref, high_ref):
         rows = ref.shape[1] // 2
-        values.append(
-            sum(
-                product(strided(ref, core, 0, rows, 2), sooner[core])
-                + product(strided(ref, core, 1, rows, 2), later[core])
-                for core in range(2)
-            )
-        )
+        values.append(sum(product(columns_of(ref, core, 0, rows), known[core]) for core in range(2)))
     out = merged(*values)
     peers, stacks, rows, lanes = sent_ref.shape
     for stack in range(stacks):
@@ -157,16 +174,18 @@
 LIMIT = 12 * 2**20
 SCALAR = pl.BlockSpec(memory_space=pltpu.SMEM)
 LOCAL = pl.BlockSpec(memory_space=pltpu.VMEM)
-
-
-def kernel(body, shapes, *args, scalars=0, **settings):
+REMOTE = pl.BlockSpec(memory_space=pltpu.HBM)
+
+
+def kernel(body, shapes, *args, scalars=0, distant=0, scratch=(), **settings):
     outs = [jax.ShapeDtypeStruct(shape, jnp.float32) for shape in shapes]
     single = len(outs) == 1
     return pl.pallas_call(
         functools.partial(body, **settings),
         out_shape=outs[0] if single else outs,
-        in_specs=[SCALAR] * scalars + [LOCAL] * (len(args) - scalars),
+        in_specs=[SCALAR] * scalars + [LOCAL] * (len(args) - scalars - distant) + [REMOTE] * distant,
         out_specs=LOCAL if single else [LOCAL] * len(outs),
+        scratch_shapes=list(scratch),
         name=body.__name__,
         compiler_params=pltpu.CompilerParams(vmem_limit_bytes=LIMIT),
     )(*args)
@@ -183,21 +202,34 @@
     panel = panel_inverse.shape[3] * block
     core = lax.axis_index(CORE).astype(jnp.int32).reshape(1)
 
-    inverse = lax.all_gather(panel_inverse.reshape(-1, block), CORE)
     strip = coupling.reshape(row_blocks * block, window)
-    sent, early = kernel(
-        begin,
-        [(peers, block, count), (panel, count)],
-        core, targets.reshape(1, count), pair_flags.reshape(1, count), strip, inverse,
-        scalars=1, block=block,
+    wanted = targets.reshape(1, count)
+    paired = pair_flags.reshape(1, count)
+    own_inverse = panel_inverse.reshape(-1, block)
+    sent = kernel(
+        begin, [(peers, block, count)],
+        *[pltpu.with_memory_space_constraint(a, pltpu.HBM) for a in (strip, wanted, paired, own_inverse)],
+        distant=4,
+        scratch=(
+            pltpu.VMEM((panel, window), jnp.float32),
+            pltpu.VMEM((1, count), jnp.int32),
+            pltpu.VMEM((1, count), jnp.int32),
+            pltpu.VMEM((1, panel, block), jnp.float32),
+            pltpu.SemaphoreType.DMA((4,)),
+        ),
     )
     pieces = exchanged(sent, PROW)
+    early = kernel(opening, [(panel, count)], core, wanted, paired, strip, scalars=1)
+    inverse = lax.all_gather(panel_inverse[0].reshape(-1, block), CORE)
     triangle = lax.all_gather(schur[: row_blocks // 2].reshape(-1, block), CORE)
     low = lax.all_gather(zslab[: zrow_blocks // 2].reshape(-1, block), CORE)
     high = lax.all_gather(zslab[zrow_blocks // 2 :].reshape(-1, block), CORE)
-    pieces, triangle, low, high = lax.optimization_barrier((pieces, triangle, low, high))
+    pieces, early, inverse, triangle, low, high = lax.optimization_barrier(
+        (pieces, early, inverse, triangle, low, high)
+    )
+    whole = lax.all_gather(jnp.sum(pieces, axis=0), CORE)
     partial_value, later = kernel(
-        coupled, [(block, count), (block, count)], pieces, triangle, block=block
+        coupled, [(block, count), (block, count)], core, whole, triangle, scalars=1, block=block
     )
     parts = exchanged(partial_value.reshape(line, -1, count), LINE)
     mine = jnp.sum(parts, axis=0)

time: 140 us -> 139 us (level)
  waiting for transfers between devices: 8.79 us -> 1.84 us
  starting transfers between devices: 3.65 us -> 7.72 us
  blocking collectives: 119 us -> 121 us
    all_to_all x1, waiting for transfers between devices: 8.79 us -> 1.84 us  [exchanged(): return lax.all_to_all(value, axis, 0, 0, tiled=True)]
    all_to_all x1, starting transfers between devices: 3.65 us -> 7.72 us  [exchanged(): return lax.all_to_all(value, axis, 0, 0, tiled=True)]
    all_gather x1 -> x2, blocking collectives: 8.98 us -> 10.1 us  [the longest x1 5.47 us: shards(): whole = lax.all_gather(jnp.sum(pieces, axis=0), CORE)]
    pallas_call x7 -> x8, Pallas kernels: 4.88 us -> 5.78 us  [kernel(): pl.pallas_call(functools.partial(body, **settings), out_shape=outs[0] if...]
where the time goes in v3:
time: 139 us; the launch traced here: 138 us
  blocking collectives  121 us (87%)
  starting transfers between devices  7.72 us (6%)
  Pallas kernels  5.78 us (4%)
  waiting for transfers between devices  1.84 us (1%)
    all_to_all x6, blocking collectives, exchanged(): return lax.all_to_all(value, axis, 0, 0, tiled=True)  98.4 us
    all_to_all x1, starting transfers between devices, exchanged(): return lax.all_to_all(value, axis, 0, 0, tiled=True)  7.72 us
    pallas_call x8, Pallas kernels, kernel(): pl.pallas_call(functools.partial(body, **settings), out_shape=outs[0] if...  5.78 us
    all_gather x1, blocking collectives, shards(): both = lax.all_gather(owned, CORE)  5.76 us
    all_gather x1, blocking collectives, shards(): whole = lax.all_gather(jnp.sum(pieces, axis=0), CORE)  5.47 us
    all_gather x1, blocking collectives, shards(): inverse = lax.all_gather(panel_inverse[0].reshape(-1, block), CORE)  4.68 us
  transfers between devices with their start and end apart: 1, of which 1 were waited for; matrix products, arithmetic and copies ran while one was open for 0% of the time, Pallas kernels for 0%

profile of v3, /device:TPU:1, one launch (start us, length us, event | category | flops | bytes accessed | tf_op | source)
XLA Modules:
  0.0 137.6 jit_solution(8183849409336203497)
XLA Ops:
  0.0 2.6 %begin.1 = f32[16,128,128]{2,1,0:T(8,128)} custom-call(f32[512,256]{1,0:T(8,128)} %bitcast.13, s32[1,128]{1,0:T(1,128)} %bitcast.20, s32[1,128]{1,0:T(1,128)} %bitcast.22, f32[512,128]{1,0:T(8,128)} %bitcast.27), custom_call_target="tpu_custom_call" | custom-call | tf_op jit(solution)/shard_map/begin/pallas_call | solution.py:183
  2.6 0.0 copy-start.3
  2.6 0.0 copy-start
  2.6 7.7 %all-to-all-start = ((f32[16,128,128]{2,1,0:T(8,128)}), f32[16,128,128]{2,1,0:T(8,128)S(1)}, u32[]{:S(2)}, u32[]{:S(2)}) async-start(f32[16,128,128]{2,1,0:T(8,128)} %begin.1), calls=%async_computation | async-start | bytes 2097152 | tf_op jit(solution)/shard_map/all_to_all | solution.py:25
  10.3 0.0 copy-done.3
  10.4 0.0 copy-start.1
  10.4 0.0 copy-start.2
  10.4 0.0 copy-done
  10.4 0.6 copy-done.1
  11.0 0.0 copy-done.2
  11.1 0.3 opening.1.early_ref
  11.4 0.0 copy-start.4
  11.4 4.7 %all_gather.24.inverse_ref = f32[2,256,128]{2,1,0:T(8,128)S(1)} all-gather(f32[1,256,128]{2,1,0:T(8,128)S(1)} %bitcast.28), channel_id=1, replica_groups=mesh['prow_0'=4,'prow_1'=4,'pcol_0'=16,'pcol_1'=2] {'pcol_1'}, dimensions={0}, use_global_device_ids=true | all-gather | bytes 393216 | tf_op jit(solution)/shard_map/all_gather | solution.py:223
  16.1 0.4 fusion
  16.5 2.2 %all_gather.26.low_ref = f32[2,512,128]{2,1,0:T(8,128)S(1)} all-gather(f32[1,512,128]{2,1,0:T(8,128)S(1)} %bitcast.26), channel_id=1, replica_groups=mesh['prow_0'=4,'prow_1'=4,'pcol_0'=16,'pcol_1'=2] {'pcol_1'}, dimensions={0}, use_global_device_ids=true | all-gather | bytes 786432 | tf_op jit(solution)/shard_map/all_gather | solution.py:225
  18.6 2.3 %all_gather.27.high_ref = f32[2,512,128]{2,1,0:T(8,128)S(1)} all-gather(f32[1,512,128]{2,1,0:T(8,128)S(1)} %bitcast.25), channel_id=1, replica_groups=mesh['prow_0'=4,'prow_1'=4,'pcol_0'=16,'pcol_1'=2] {'pcol_1'}, dimensions={0}, use_global_device_ids=true | all-gather | bytes 786432 | tf_op jit(solution)/shard_map/all_gather | solution.py:226
  21.0 2.2 %all_gather.25.triangle_ref = f32[2,512,128]{2,1,0:T(8,128)S(1)} all-gather(f32[1,512,128]{2,1,0:T(8,128)S(1)} %bitcast.24), channel_id=1, replica_groups=mesh['prow_0'=4,'prow_1'=4,'pcol_0'=16,'pcol_1'=2] {'pcol_1'}, dimensions={0}, use_global_device_ids=true | all-gather | bytes 786432 | tf_op jit(solution)/shard_map/all_gather | solution.py:224
  23.1 1.8 %all-to-all-done = f32[16,128,128]{2,1,0:T(8,128)S(1)} async-done(((f32[16,128,128]{2,1,0:T(8,128)}), f32[16,128,128]{2,1,0:T(8,128)S(1)}, u32[]{:S(2)}, u32[]{:S(2)}) %all-to-all-start) | async-done | bytes 1048608 | tf_op jit(solution)/shard_map/all_to_all | solution.py:25
  25.0 0.1 reduce_sum.27
  25.0 5.5 %all-gather = f32[256,128]{1,0:T(8,128)S(1)} all-gather(f32[128,128]{1,0:T(8,128)S(1)} %reduce_sum.27), channel_id=2, replica_groups=mesh['prow_0'=4,'prow_1'=4,'pcol_0'=16,'pcol_1'=2] {'pcol_1'}, dimensions={0}, use_global_device_ids=true | all-gather | bytes 196608 | tf_op jit(solution)/shard_map/all_gather | solution.py:230
  30.5 0.4 coupled.1
  30.9 26.5 %all_to_all.35 = f32[16,8,128]{2,1,0:T(8,128)S(1)} all-to-all(f32[16,8,128]{2,1,0:T(8,128)S(1)} %bitcast.19), channel_id=1, replica_groups=mesh['prow_0'=4,'prow_1'=4,'pcol_0'=16,'pcol_1'=2] {'pcol_0'}, dimensions={0} | all-to-all | bytes 131072 | tf_op jit(solution)/shard_map/all_to_all | solution.py:25
  57.5 15.3 %all_to_all.36 = f32[16,8,128]{2,1,0:T(8,128)S(1)} all-to-all(f32[16,8,128]{2,1,0:T(8,128)S(1)} %broadcast_in_dim.2), channel_id=1, replica_groups=mesh['prow_0'=4,'prow_1'=4,'pcol_0'=16,'pcol_1'=2] {'pcol_0'}, dimensions={0} | all-to-all | bytes 131072 | tf_op jit(solution)/shard_map/all_to_all | solution.py:25
  72.7 0.5 solved.1
  73.2 18.2 %all_to_all.37.pieces_ref = f32[16,128,128]{2,1,0:T(8,128)S(1)} all-to-all(f32[16,128,128]{2,1,0:T(8,128)S(1)} %solved.1), channel_id=1, replica_groups=mesh['prow_0'=4,'prow_1'=4,'pcol_0'=16,'pcol_1'=2] {'prow_0','prow_1'}, dimensions={0} | all-to-all | bytes 2097152 | tf_op jit(solution)/shard_map/all_to_all | solution.py:25
  91.4 1.1 carried.1
  92.5 14.7 %all_to_all.38 = f32[16,2,8,128]{3,2,1,0:T(8,128)S(1)} all-to-all(f32[16,2,8,128]{3,2,1,0:T(8,128)S(1)} %carried.1), channel_id=1, replica_groups=mesh['prow_0'=4,'prow_1'=4,'pcol_0'=16,'pcol_1'=2] {'pcol_0'}, dimensions={0} | all-to-all | bytes 262144 | tf_op jit(solution)/shard_map/all_to_all | solution.py:25
  107.3 5.8 %all-gather.1 = f32[4,8,128]{2,1,0:T(8,128)S(1)} all-gather(f32[2,8,128]{2,1,0:T(8,128)S(1)} %reduce_sum.29), channel_id=3, replica_groups=mesh['prow_0'=4,'prow_1'=4,'pcol_0'=16,'pcol_1'=2] {'pcol_1'}, dimensions={0}, use_global_device_ids=true | all-gather | bytes 24576 | tf_op jit(solution)/shard_map/all_gather | solution.py:245
  113.0 0.1 squared.1
  113.1 14.7 %all_to_all.39.pieces_ref = f32[16,1,128]{2,1,0:T(1,128)S(1)} all-to-all(f32[16,1,128]{2,1,0:T(1,128)S(1)} %squared.1), channel_id=1, replica_groups=mesh['prow_0'=4,'prow_1'=4,'pcol_0'=16,'pcol_1'=2] {'pcol_0'}, dimensions={0} | all-to-all | bytes 16384 | tf_op jit(solution)/shard_map/all_to_all | solution.py:25
  127.9 9.1 %all_to_all.40.pieces_ref = f32[16,1,128]{2,1,0:T(1,128)S(1)} all-to-all(f32[16,1,128]{2,1,0:T(1,128)S(1)} %again.1), channel_id=1, replica_groups=mesh['prow_0'=4,'prow_1'=4,'pcol_0'=16,'pcol_1'=2] {'prow_0','prow_1'}, dimensions={0} | all-to-all | bytes 16384 | tf_op jit(solution)/shard_map/all_to_all | solution.py:25
  136.9 0.7 finished.1
  (8 shorter events, 0.1 us)
Async XLA Ops:
  2.6 7.8 %copy-start.3 = (f32[2,1,128,2,1,128]{5,4,3,2,1,0:T(1,128)S(1)}, f32[2,1,128,2,1,128]{5,4,3,2,1,0:T(1,128)}, u32[]{:S(2)}) copy-start(f32[2,1,128,2,1,128]{5,4,3,2,1,0:T(1,128)} %param.7) | copy-start | bytes 786436
  2.6 7.8 %copy-start = (f32[4,1,128,256]{3,2,1,0:T(8,128)S(1)}, f32[4,1,128,256]{3,2,1,0:T(8,128)}, u32[]{:S(2)}) copy-start(f32[4,1,128,256]{3,2,1,0:T(8,128)} %param.8) | copy-start | bytes 1572868
  2.6 22.3 %all-to-all-start = ((f32[16,128,128]{2,1,0:T(8,128)}), f32[16,128,128]{2,1,0:T(8,128)S(1)}, u32[]{:S(2)}, u32[]{:S(2)}) async-start(f32[16,128,128]{2,1,0:T(8,128)} %begin.1), calls=%async_computation | async-start | bytes 2097152 | tf_op jit(solution)/shard_map/all_to_all | solution.py:25
  10.4 0.7 copy-start.1
  10.4 0.7 copy-start.2
  11.4 4.7 %copy-start.4 = (f32[4,1,128,2,1,128]{5,4,3,2,1,0:T(1,128)S(1)}, f32[4,1,128,2,1,128]{5,4,3,2,1,0:T(1,128)}, u32[]{:S(2)}) copy-start(f32[4,1,128,2,1,128]{5,4,3,2,1,0:T(1,128)} %param.9) | copy-start | bytes 1572868
  18.6 2.3 %slice-start = ((f32[4,1,128,2,1,128]{5,4,3,2,1,0:T(1,128)}), f32[2,1,128,2,1,128]{5,4,3,2,1,0:T(1,128)S(1)}, s32[]{:S(2)}) async-start(f32[4,1,128,2,1,128]{5,4,3,2,1,0:T(1,128)} %param.6), calls=%async_computation.7 | async-start | bytes 524288 | tf_op jit(solution)/shard_map/slice | solution.py:224

commit v4 on v3

--- a/solution.py
+++ b/solution.py
@@ -8,21 +8,41 @@
 from jax.sharding import Mesh
 from jax.sharding import PartitionSpec as P
 
-PROW = ("prow_0", "prow_1")
-PCOL = ("pcol_0", "pcol_1")
+ROWS = ("prow_0", "prow_1", "prow_2", "prow_3")
 LINE = "pcol_0"
 CORE = "pcol_1"
+PCOL = (LINE, CORE)
 
 
 EPSILON = 1e-06
+
+FIRST = {"prow_0": 1, "prow_1": 0, "prow_2": 1, "prow_3": 0, "pcol_0": 8, "pcol_1": 0}
 
 
 def product(left, right):
     return jnp.dot(left, right, precision=lax.Precision.HIGHEST, preferred_element_type=jnp.float32)
 
 
+def in_turn(first, sizes):
+    order = [0]
+    for start, size in zip(first, sizes, strict=True):
+        order = [place * size + (start + step) % size for place in order for step in range(size)]
+    return [order]
+
+
 def exchanged(value, axis):
-    return lax.all_to_all(value, axis, 0, 0, tiled=True)
+    names = (axis,) if isinstance(axis, str) else axis
+    order = in_turn([FIRST[name] for name in names], [lax.axis_size(name) for name in names])
+    return lax.all_to_all(value, axis, 0, 0, tiled=True, axis_index_groups=order)
+
+
+def from_everyone(value, axis):
+    size = lax.axis_size(axis)
+    return exchanged(jnp.broadcast_to(value[None], (size, *value.shape)), axis)
+
+
+def in_pairs(value, near, others):
+    return from_everyone(jnp.sum(lax.all_gather(value, near), axis=0), others)
 
 
 def first_half(shape):
@@ -125,9 +145,9 @@
 
 def solved(summed_ref, early_ref, inverse_ref, sent_ref, *, block):
     residual = early_ref[...] - jnp.concatenate(doubled(summed_ref[...]), axis=0)
-    out = merged(*[product(columns_of(inverse_ref, core, 0, block), residual) for core in range(2)])
-    for peer in range(sent_ref.shape[0]):
-        sent_ref[peer] = out
+    sent_ref[...] = merged(
+        *[product(columns_of(inverse_ref, core, 0, block), residual) for core in range(2)]
+    )
 
 
 def carried(pieces_ref, later_ref, low_ref, high_ref, sent_ref, *, block):
@@ -140,8 +160,12 @@
         values.append(sum(product(columns_of(ref, core, 0, rows), known[core]) for core in range(2)))
     out = merged(*values)
     peers, stacks, rows, lanes = sent_ref.shape
+    first = FIRST[LINE]
     for stack in range(stacks):
-        sent_ref[:, stack] = out[stack * block : (stack + 1) * block].reshape(peers, rows, lanes)
+        shares = out[stack * block : (stack + 1) * block].reshape(peers, rows, lanes)
+        sent_ref[: peers - first, stack] = shares[first:]
+        if first:
+            sent_ref[peers - first :, stack] = shares[:first]
 
 
 def squared(both_ref, sent_ref):
@@ -198,7 +222,7 @@
     zrow_blocks = zslab.shape[0]
     count = targets.shape[0]
     line = lax.axis_size(LINE)
-    peers = lax.axis_size(PROW)
+    peers = lax.axis_size(ROWS)
     panel = panel_inverse.shape[3] * block
     core = lax.axis_index(CORE).astype(jnp.int32).reshape(1)
 
@@ -218,7 +242,7 @@
             pltpu.SemaphoreType.DMA((4,)),
         ),
     )
-    pieces = exchanged(sent, PROW)
+    pieces = exchanged(sent, ROWS)
     early = kernel(opening, [(panel, count)], core, wanted, paired, strip, scalars=1)
     inverse = lax.all_gather(panel_inverse[0].reshape(-1, block), CORE)
     triangle = lax.all_gather(schur[: row_blocks // 2].reshape(-1, block), CORE)
@@ -234,8 +258,8 @@
     parts = exchanged(partial_value.reshape(line, -1, count), LINE)
     mine = jnp.sum(parts, axis=0)
     summed = exchanged(jnp.broadcast_to(mine[None], (line, *mine.shape)), LINE).reshape(block, count)
-    sent = kernel(solved, [(peers, block, count)], summed, early, inverse, block=block)
-    pieces = exchanged(sent, PROW)
+    applied = kernel(solved, [(block, count)], summed, early, inverse, block=block)
+    pieces = in_pairs(applied, ROWS[3], ROWS[:3])
     stacked = kernel(
         carried,
         [(line, zrow_blocks // 2, block // line, count)],
@@ -244,7 +268,7 @@
     owned = jnp.sum(exchanged(stacked, LINE), axis=0)
     both = lax.all_gather(owned, CORE)
     squares = exchanged(kernel(squared, [(line, 1, count)], both), LINE)
-    squares = exchanged(kernel(again, [(peers, 1, count)], squares), PROW)
+    squares = exchanged(kernel(again, [(peers, 1, count)], squares), ROWS)
     total = zrow_blocks * block * peers
     rows = block // line // lax.axis_size(CORE)
     return kernel(
@@ -253,15 +277,15 @@
 
 
 def solution(mesh):
-    split = Mesh(mesh.devices.reshape(4, 4, 16, 2), ("prow_0", "prow_1", "pcol_0", "pcol_1"))
+    split = Mesh(mesh.devices.reshape(2, 2, 2, 2, 16, 2), (*ROWS, *PCOL))
     placed = (
-        P(None, PROW, None, None, PCOL, None),
-        P(None, PCOL, None, None, PROW, None),
-        P(None, PROW, None, None),
-        P(None, PROW, None, None, PCOL, None),
+        P(None, ROWS, None, None, PCOL, None),
+        P(None, PCOL, None, None, ROWS, None),
+        P(None, ROWS, None, None),
+        P(None, ROWS, None, None, PCOL, None),
         P(),
         P(),
     )
     return jax.shard_map(
-        shards, mesh=split, in_specs=placed, out_specs=P(None, PROW, PCOL, None), check_vma=False
-    )
+        shards, mesh=split, in_specs=placed, out_specs=P(None, ROWS, PCOL, None), check_vma=False
+    )

time: 139 us -> 129 us (0.928)
  blocking collectives: 121 us -> 110 us
  starting transfers between devices: 7.72 us -> 9.84 us
  waiting for transfers between devices: 1.84 us -> 0.01 us
    all_to_all x6, blocking collectives: 98.4 us -> 84.6 us  [exchanged(): lax.all_to_all(value, axis, 0, 0, tiled=True, axis_index_groups=order)]
    all_gather x0 -> x1, blocking collectives: none -> 3.78 us  [in_pairs(): return from_everyone(jnp.sum(lax.all_gather(value, near), axis=0), others)]
    all_gather x1, blocking collectives: 5.47 us -> 1.91 us  [shards(): whole = lax.all_gather(jnp.sum(pieces, axis=0), CORE)]
    all_to_all x1, starting transfers between devices: 7.72 us -> 9.84 us  [exchanged(): lax.all_to_all(value, axis, 0, 0, tiled=True, axis_index_groups=order)]
    all_to_all x1, waiting for transfers between devices: 1.84 us -> 0.01 us  [exchanged(): lax.all_to_all(value, axis, 0, 0, tiled=True, axis_index_groups=order)]
    all_gather x1, blocking collectives: 4.68 us -> 6.13 us  [shards(): inverse = lax.all_gather(panel_inverse[0].reshape(-1, block), CORE)]
  transfers between devices with their start and end apart: 1 -> 1, of which waited for: 1 -> 0; matrix products, arithmetic and copies ran while one was open for 0% -> 0% of each run, Pallas kernels for 0% -> 0%
where the time goes in v4:
time: 129 us; the launch traced here: 127 us
  blocking collectives  110 us (85%)
  starting transfers between devices  9.84 us (8%)
  Pallas kernels  5.71 us (4%)
    all_to_all x6, blocking collectives, exchanged(): lax.all_to_all(value, axis, 0, 0, tiled=True, axis_index_groups=order)  84.6 us
    all_to_all x1, starting transfers between devices, exchanged(): lax.all_to_all(value, axis, 0, 0, tiled=True, axis_index_groups=order)  9.84 us
    all_gather x1, blocking collectives, shards(): both = lax.all_gather(owned, CORE)  6.9 us
    all_gather x1, blocking collectives, shards(): inverse = lax.all_gather(panel_inverse[0].reshape(-1, block), CORE)  6.13 us
    pallas_call x8, Pallas kernels, kernel(): pl.pallas_call(functools.partial(body, **settings), out_shape=outs[0] if...  5.71 us
    all_gather x1, blocking collectives, in_pairs(): return from_everyone(jnp.sum(lax.all_gather(value, near), axis=0), others)  3.78 us
  transfers between devices with their start and end apart: 1, of which 0 were waited for; matrix products, arithmetic and copies ran while one was open for 0% of the time, Pallas kernels for 0%

profile of v4, /device:TPU:1, one launch (start us, length us, event | category | flops | bytes accessed | tf_op | source)
XLA Modules:
  0.0 126.9 jit_solution(3905303120440931905)
XLA Ops:
  0.0 2.6 %begin.1 = f32[16,128,128]{2,1,0:T(8,128)} custom-call(f32[512,256]{1,0:T(8,128)} %bitcast.14, s32[1,128]{1,0:T(1,128)} %bitcast.21, s32[1,128]{1,0:T(1,128)} %bitcast.23, f32[512,128]{1,0:T(8,128)} %bitcast.28), custom_call_target="tpu_custom_call" | custom-call | tf_op jit(solution)/shard_map/begin/pallas_call | solution.py:207
  2.6 0.0 copy-start.3
  2.6 0.0 copy-start
  2.6 9.8 %all-to-all-start = ((f32[16,128,128]{2,1,0:T(8,128)}), f32[16,128,128]{2,1,0:T(8,128)S(1)}, u32[]{:S(2)}, u32[]{:S(2)}) async-start(f32[16,128,128]{2,1,0:T(8,128)} %begin.1), calls=%async_computation | async-start | bytes 2097152 | tf_op jit(solution)/shard_map/all_to_all | solution.py:36
  12.5 0.0 copy-done.3
  12.5 0.0 copy-start.1
  12.5 0.0 copy-start.2
  12.5 0.6 copy-done.1
  13.2 0.0 copy-done.2
  13.2 0.3 opening.1.early_ref
  13.5 0.0 copy-start.4
  13.5 6.1 %all_gather.30.inverse_ref = f32[2,256,128]{2,1,0:T(8,128)S(1)} all-gather(f32[1,256,128]{2,1,0:T(8,128)S(1)} %bitcast.29), channel_id=1, replica_groups=mesh['prow_0'=2,'prow_1'=2,'prow_2'=2,'prow_3'=2,'pcol_0'=16,'pcol_1'=2]..., dimensions={0}, use_global_device_ids=true | all-gather | bytes 393216 | tf_op jit(solution)/shard_map/all_gather | solution.py:247
  19.7 0.4 fusion
  20.0 2.2 %all_gather.32.low_ref = f32[2,512,128]{2,1,0:T(8,128)S(1)} all-gather(f32[1,512,128]{2,1,0:T(8,128)S(1)} %bitcast.27), channel_id=1, replica_groups=mesh['prow_0'=2,'prow_1'=2,'prow_2'=2,'prow_3'=2,'pcol_0'=16,'pcol_1'=2]..., dimensions={0}, use_global_device_ids=true | all-gather | bytes 786432 | tf_op jit(solution)/shard_map/all_gather | solution.py:249
  22.2 2.3 %all_gather.33.high_ref = f32[2,512,128]{2,1,0:T(8,128)S(1)} all-gather(f32[1,512,128]{2,1,0:T(8,128)S(1)} %bitcast.26), channel_id=1, replica_groups=mesh['prow_0'=2,'prow_1'=2,'prow_2'=2,'prow_3'=2,'pcol_0'=16,'pcol_1'=2]..., dimensions={0}, use_global_device_ids=true | all-gather | bytes 786432 | tf_op jit(solution)/shard_map/all_gather | solution.py:250
  24.5 2.2 %all_gather.31.triangle_ref = f32[2,512,128]{2,1,0:T(8,128)S(1)} all-gather(f32[1,512,128]{2,1,0:T(8,128)S(1)} %bitcast.25), channel_id=1, replica_groups=mesh['prow_0'=2,'prow_1'=2,'prow_2'=2,'prow_3'=2,'pcol_0'=16,'pcol_1'=2]..., dimensions={0}, use_global_device_ids=true | all-gather | bytes 786432 | tf_op jit(solution)/shard_map/all_gather | solution.py:248
  26.7 0.0 all-to-all-done
  26.7 0.1 reduce_sum.36
  26.8 1.9 %all-gather = f32[256,128]{1,0:T(8,128)S(1)} all-gather(f32[128,128]{1,0:T(8,128)S(1)} %reduce_sum.36), channel_id=2, replica_groups=mesh['prow_0'=2,'prow_1'=2,'prow_2'=2,'prow_3'=2,'pcol_0'=16,'pcol_1'=2]..., dimensions={0}, use_global_device_ids=true | all-gather | bytes 196608 | tf_op jit(solution)/shard_map/all_gather | solution.py:254
  28.7 0.4 coupled.1
  29.1 21.1 %all_to_all.35 = f32[16,8,128]{2,1,0:T(8,128)S(1)} all-to-all(f32[16,8,128]{2,1,0:T(8,128)S(1)} %bitcast.20), channel_id=1, replica_groups={{16,18,20,22,24,26,28,30,0,2,4,6,8,10,12,14},{17,19,21,23,25,27,29,31,1..., dimensions={0} | all-to-all | bytes 131072 | tf_op jit(solution)/shard_map/all_to_all | solution.py:36
  50.2 14.4 %all_to_all.36 = f32[16,8,128]{2,1,0:T(8,128)S(1)} all-to-all(f32[16,8,128]{2,1,0:T(8,128)S(1)} %broadcast_in_dim.4), channel_id=1, replica_groups={{16,18,20,22,24,26,28,30,0,2,4,6,8,10,12,14},{17,19,21,23,25,27,29,31,1..., dimensions={0} | all-to-all | bytes 131072 | tf_op jit(solution)/shard_map/all_to_all | solution.py:36
  64.7 0.4 solved.1
  65.1 3.8 %all-gather.1 = f32[256,128]{1,0:T(8,128)S(1)} all-gather(f32[128,128]{1,0:T(8,128)S(1)} %solved.1), channel_id=3, replica_groups=mesh['prow_0'=2,'prow_1'=2,'prow_2'=2,'prow_3'=2,'pcol_0'=16,'pcol_1'=2]..., dimensions={0}, use_global_device_ids=true | all-gather | bytes 196608 | tf_op jit(solution)/shard_map/all_gather | solution.py:45
  68.9 11.3 %all_to_all.37.pieces_ref = f32[8,128,128]{2,1,0:T(8,128)S(1)} all-to-all(f32[8,128,128]{2,1,0:T(8,128)S(1)} %broadcast_in_dim.5), channel_id=1, replica_groups={{320,256,448,384,64,0,192,128},{321,257,449,385,65,1,193,129},{322,258,..., dimensions={0} | all-to-all | bytes 1048576 | tf_op jit(solution)/shard_map/all_to_all | solution.py:36
  80.3 1.1 carried.1
  81.4 16.1 %all_to_all.38 = f32[16,2,8,128]{3,2,1,0:T(8,128)S(1)} all-to-all(f32[16,2,8,128]{3,2,1,0:T(8,128)S(1)} %carried.1), channel_id=1, replica_groups={{16,18,20,22,24,26,28,30,0,2,4,6,8,10,12,14},{17,19,21,23,25,27,29,31,1..., dimensions={0} | all-to-all | bytes 262144 | tf_op jit(solution)/shard_map/all_to_all | solution.py:36
  97.4 6.9 %all-gather.2 = f32[4,8,128]{2,1,0:T(8,128)S(1)} all-gather(f32[2,8,128]{2,1,0:T(8,128)S(1)} %reduce_sum.39), channel_id=4, replica_groups=mesh['prow_0'=2,'prow_1'=2,'prow_2'=2,'prow_3'=2,'pcol_0'=16,'pcol_1'=2]..., dimensions={0}, use_global_device_ids=true | all-gather | bytes 24576 | tf_op jit(solution)/shard_map/all_gather | solution.py:269
  104.3 0.1 squared.1
  104.4 12.8 %all_to_all.39.pieces_ref = f32[16,1,128]{2,1,0:T(1,128)S(1)} all-to-all(f32[16,1,128]{2,1,0:T(1,128)S(1)} %squared.1), channel_id=1, replica_groups={{16,18,20,22,24,26,28,30,0,2,4,6,8,10,12,14},{17,19,21,23,25,27,29,31,1..., dimensions={0} | all-to-all | bytes 16384 | tf_op jit(solution)/shard_map/all_to_all | solution.py:36
  117.3 8.9 %all_to_all.40.pieces_ref = f32[16,1,128]{2,1,0:T(1,128)S(1)} all-to-all(f32[16,1,128]{2,1,0:T(1,128)S(1)} %again.1), channel_id=1, replica_groups={{320,352,256,288,448,480,384,416,64,96,0,32,192,224,128,160},{321,353,2..., dimensions={0} | all-to-all | bytes 16384 | tf_op jit(solution)/shard_map/all_to_all | solution.py:36
  126.2 0.7 finished.1
  (11 shorter events, 0.1 us)
Async XLA Ops:
  2.6 9.9 %copy-start.3 = (f32[2,1,128,2,1,128]{5,4,3,2,1,0:T(1,128)S(1)}, f32[2,1,128,2,1,128]{5,4,3,2,1,0:T(1,128)}, u32[]{:S(2)}) copy-start(f32[2,1,128,2,1,128]{5,4,3,2,1,0:T(1,128)} %param.7) | copy-start | bytes 786436
  2.6 9.9 %copy-start = (f32[4,1,128,256]{3,2,1,0:T(8,128)S(1)}, f32[4,1,128,256]{3,2,1,0:T(8,128)}, u32[]{:S(2)}) copy-start(f32[4,1,128,256]{3,2,1,0:T(8,128)} %param.8) | copy-start | bytes 1572868
  2.6 24.1 %all-to-all-start = ((f32[16,128,128]{2,1,0:T(8,128)}), f32[16,128,128]{2,1,0:T(8,128)S(1)}, u32[]{:S(2)}, u32[]{:S(2)}) async-start(f32[16,128,128]{2,1,0:T(8,128)} %begin.1), calls=%async_computation | async-start | bytes 2097152 | tf_op jit(solution)/shard_map/all_to_all | solution.py:36
  12.5 0.7 copy-start.1
  12.5 0.7 copy-start.2
  13.5 6.1 %copy-start.4 = (f32[4,1,128,2,1,128]{5,4,3,2,1,0:T(1,128)S(1)}, f32[4,1,128,2,1,128]{5,4,3,2,1,0:T(1,128)}, u32[]{:S(2)}) copy-start(f32[4,1,128,2,1,128]{5,4,3,2,1,0:T(1,128)} %param.9) | copy-start | bytes 1572868
  22.2 2.3 %slice-start = ((f32[4,1,128,2,1,128]{5,4,3,2,1,0:T(1,128)}), f32[2,1,128,2,1,128]{5,4,3,2,1,0:T(1,128)S(1)}, s32[]{:S(2)}) async-start(f32[4,1,128,2,1,128]{5,4,3,2,1,0:T(1,128)} %param.6), calls=%async_computation.7 | async-start | bytes 524288 | tf_op jit(solution)/shard_map/slice | solution.py:248

commit v5 on v4

--- a/solution.py
+++ b/solution.py
@@ -30,6 +30,22 @@
     return [order]
 
 
+def across_pairs():
+    size = lax.axis_size(ROWS[2]) * lax.axis_size(ROWS[3])
+    rows = lax.axis_size(ROWS[0]) * lax.axis_size(ROWS[1])
+    first = rows // 2
+    return [
+        [(first + step) % rows * size + column for step in range(rows) for column in columns]
+        for columns in ((2, 1), (3, 0))
+    ]
+
+
+def to_all_pairs(value):
+    groups = across_pairs()
+    sent = jnp.broadcast_to(value[None], (len(groups[0]), *value.shape))
+    return lax.all_to_all(sent, ROWS, 0, 0, tiled=True, axis_index_groups=groups)
+
+
 def exchanged(value, axis):
     names = (axis,) if isinstance(axis, str) else axis
     order = in_turn([FIRST[name] for name in names], [lax.axis_size(name) for name in names])
@@ -41,8 +57,8 @@
     return exchanged(jnp.broadcast_to(value[None], (size, *value.shape)), axis)
 
 
-def in_pairs(value, near, others):
-    return from_everyone(jnp.sum(lax.all_gather(value, near), axis=0), others)
+def in_pairs(value, near):
+    return to_all_pairs(jnp.sum(lax.all_gather(value, near), axis=0))
 
 
 def first_half(shape):
@@ -259,7 +275,7 @@
     mine = jnp.sum(parts, axis=0)
     summed = exchanged(jnp.broadcast_to(mine[None], (line, *mine.shape)), LINE).reshape(block, count)
     applied = kernel(solved, [(block, count)], summed, early, inverse, block=block)
-    pieces = in_pairs(applied, ROWS[3], ROWS[:3])
+    pieces = in_pairs(applied, ROWS[3])
     stacked = kernel(
         carried,
         [(line, zrow_blocks // 2, block // line, count)],

time: 129 us -> 129 us (level)
    all_to_all x6 -> x5, blocking collectives: 84.6 us -> 73.2 us  [exchanged(): lax.all_to_all(value, axis, 0, 0, tiled=True, axis_index_groups=order)]
    all_to_all x0 -> x1, blocking collectives: none -> 11 us  [to_all_pairs(): lax.all_to_all(sent, ROWS, 0, 0, tiled=True, axis_index_groups=groups)]
where the time goes in v5:
time: 129 us; the launch traced here: 126 us
  blocking collectives  110 us (85%)
  starting transfers between devices  9.84 us (8%)
  Pallas kernels  5.71 us (4%)
    all_to_all x5, blocking collectives, exchanged(): lax.all_to_all(value, axis, 0, 0, tiled=True, axis_index_groups=order)  73.2 us
    all_to_all x1, blocking collectives, to_all_pairs(): lax.all_to_all(sent, ROWS, 0, 0, tiled=True, axis_index_groups=groups)  11 us
    all_to_all x1, starting transfers between devices, exchanged(): lax.all_to_all(value, axis, 0, 0, tiled=True, axis_index_groups=order)  9.84 us
    all_gather x1, blocking collectives, shards(): both = lax.all_gather(owned, CORE)  6.9 us
    all_gather x1, blocking collectives, shards(): inverse = lax.all_gather(panel_inverse[0].reshape(-1, block), CORE)  6.13 us
    pallas_call x8, Pallas kernels, kernel(): pl.pallas_call(functools.partial(body, **settings), out_shape=outs[0] if...  5.71 us
    all_gather x1, blocking collectives, in_pairs(): return to_all_pairs(jnp.sum(lax.all_gather(value, near), axis=0))  3.78 us
  transfers between devices with their start and end apart: 1, of which 0 were waited for; matrix products, arithmetic and copies ran while one was open for 0% of the time, Pallas kernels for 0%

profile of v5, /device:TPU:1, one launch (start us, length us, event | category | flops | bytes accessed | tf_op | source)
XLA Modules:
  0.0 126.5 jit_solution(536785169983022592)
XLA Ops:
  0.0 2.6 %begin.1 = f32[16,128,128]{2,1,0:T(8,128)} custom-call(f32[512,256]{1,0:T(8,128)} %bitcast.14, s32[1,128]{1,0:T(1,128)} %bitcast.21, s32[1,128]{1,0:T(1,128)} %bitcast.23, f32[512,128]{1,0:T(8,128)} %bitcast.28), custom_call_target="tpu_custom_call" | custom-call | tf_op jit(solution)/shard_map/begin/pallas_call | solution.py:223
  2.6 0.0 copy-start.3
  2.6 0.0 copy-start
  2.6 9.8 %all-to-all-start = ((f32[16,128,128]{2,1,0:T(8,128)}), f32[16,128,128]{2,1,0:T(8,128)S(1)}, u32[]{:S(2)}, u32[]{:S(2)}) async-start(f32[16,128,128]{2,1,0:T(8,128)} %begin.1), calls=%async_computation | async-start | bytes 2097152 | tf_op jit(solution)/shard_map/all_to_all | solution.py:52
  12.5 0.0 copy-done.3
  12.5 0.0 copy-start.1
  12.5 0.0 copy-start.2
  12.5 0.6 copy-done.1
  13.2 0.0 copy-done.2
  13.2 0.3 opening.1.early_ref
  13.5 0.0 copy-start.4
  13.5 6.1 %all_gather.30.inverse_ref = f32[2,256,128]{2,1,0:T(8,128)S(1)} all-gather(f32[1,256,128]{2,1,0:T(8,128)S(1)} %bitcast.29), channel_id=1, replica_groups=mesh['prow_0'=2,'prow_1'=2,'prow_2'=2,'prow_3'=2,'pcol_0'=16,'pcol_1'=2]..., dimensions={0}, use_global_device_ids=true | all-gather | bytes 393216 | tf_op jit(solution)/shard_map/all_gather | solution.py:263
  19.7 0.4 fusion
  20.0 2.2 %all_gather.32.low_ref = f32[2,512,128]{2,1,0:T(8,128)S(1)} all-gather(f32[1,512,128]{2,1,0:T(8,128)S(1)} %bitcast.27), channel_id=1, replica_groups=mesh['prow_0'=2,'prow_1'=2,'prow_2'=2,'prow_3'=2,'pcol_0'=16,'pcol_1'=2]..., dimensions={0}, use_global_device_ids=true | all-gather | bytes 786432 | tf_op jit(solution)/shard_map/all_gather | solution.py:265
  22.2 2.3 %all_gather.33.high_ref = f32[2,512,128]{2,1,0:T(8,128)S(1)} all-gather(f32[1,512,128]{2,1,0:T(8,128)S(1)} %bitcast.26), channel_id=1, replica_groups=mesh['prow_0'=2,'prow_1'=2,'prow_2'=2,'prow_3'=2,'pcol_0'=16,'pcol_1'=2]..., dimensions={0}, use_global_device_ids=true | all-gather | bytes 786432 | tf_op jit(solution)/shard_map/all_gather | solution.py:266
  24.5 2.2 %all_gather.31.triangle_ref = f32[2,512,128]{2,1,0:T(8,128)S(1)} all-gather(f32[1,512,128]{2,1,0:T(8,128)S(1)} %bitcast.25), channel_id=1, replica_groups=mesh['prow_0'=2,'prow_1'=2,'prow_2'=2,'prow_3'=2,'pcol_0'=16,'pcol_1'=2]..., dimensions={0}, use_global_device_ids=true | all-gather | bytes 786432 | tf_op jit(solution)/shard_map/all_gather | solution.py:264
  26.7 0.0 all-to-all-done
  26.7 0.1 reduce_sum.36
  26.8 1.9 %all-gather = f32[256,128]{1,0:T(8,128)S(1)} all-gather(f32[128,128]{1,0:T(8,128)S(1)} %reduce_sum.36), channel_id=2, replica_groups=mesh['prow_0'=2,'prow_1'=2,'prow_2'=2,'prow_3'=2,'pcol_0'=16,'pcol_1'=2]..., dimensions={0}, use_global_device_ids=true | all-gather | bytes 196608 | tf_op jit(solution)/shard_map/all_gather | solution.py:270
  28.7 0.4 coupled.1
  29.1 21.1 %all_to_all.35 = f32[16,8,128]{2,1,0:T(8,128)S(1)} all-to-all(f32[16,8,128]{2,1,0:T(8,128)S(1)} %bitcast.20), channel_id=1, replica_groups={{16,18,20,22,24,26,28,30,0,2,4,6,8,10,12,14},{17,19,21,23,25,27,29,31,1..., dimensions={0} | all-to-all | bytes 131072 | tf_op jit(solution)/shard_map/all_to_all | solution.py:52
  50.2 14.4 %all_to_all.36 = f32[16,8,128]{2,1,0:T(8,128)S(1)} all-to-all(f32[16,8,128]{2,1,0:T(8,128)S(1)} %broadcast_in_dim.4), channel_id=1, replica_groups={{16,18,20,22,24,26,28,30,0,2,4,6,8,10,12,14},{17,19,21,23,25,27,29,31,1..., dimensions={0} | all-to-all | bytes 131072 | tf_op jit(solution)/shard_map/all_to_all | solution.py:52
  64.7 0.4 solved.1
  65.1 3.8 %all-gather.1 = f32[256,128]{1,0:T(8,128)S(1)} all-gather(f32[128,128]{1,0:T(8,128)S(1)} %solved.1), channel_id=3, replica_groups=mesh['prow_0'=2,'prow_1'=2,'prow_2'=2,'prow_3'=2,'pcol_0'=16,'pcol_1'=2]..., dimensions={0}, use_global_device_ids=true | all-gather | bytes 196608 | tf_op jit(solution)/shard_map/all_gather | solution.py:61
  68.9 11.0 %all_to_all.37.pieces_ref = f32[8,128,128]{2,1,0:T(8,128)S(1)} all-to-all(f32[8,128,128]{2,1,0:T(8,128)S(1)} %broadcast_in_dim.5), channel_id=1, replica_groups={{320,288,448,416,64,32,192,160},{352,256,480,384,96,0,224,128},{321,289..., dimensions={0} | all-to-all | bytes 1048576 | tf_op jit(solution)/shard_map/all_to_all | solution.py:46
  80.0 1.1 carried.1
  81.1 16.1 %all_to_all.38 = f32[16,2,8,128]{3,2,1,0:T(8,128)S(1)} all-to-all(f32[16,2,8,128]{3,2,1,0:T(8,128)S(1)} %carried.1), channel_id=1, replica_groups={{16,18,20,22,24,26,28,30,0,2,4,6,8,10,12,14},{17,19,21,23,25,27,29,31,1..., dimensions={0} | all-to-all | bytes 262144 | tf_op jit(solution)/shard_map/all_to_all | solution.py:52
  97.1 6.9 %all-gather.2 = f32[4,8,128]{2,1,0:T(8,128)S(1)} all-gather(f32[2,8,128]{2,1,0:T(8,128)S(1)} %reduce_sum.39), channel_id=4, replica_groups=mesh['prow_0'=2,'prow_1'=2,'prow_2'=2,'prow_3'=2,'pcol_0'=16,'pcol_1'=2]..., dimensions={0}, use_global_device_ids=true | all-gather | bytes 24576 | tf_op jit(solution)/shard_map/all_gather | solution.py:285
  104.0 0.1 squared.1
  104.1 12.8 %all_to_all.39.pieces_ref = f32[16,1,128]{2,1,0:T(1,128)S(1)} all-to-all(f32[16,1,128]{2,1,0:T(1,128)S(1)} %squared.1), channel_id=1, replica_groups={{16,18,20,22,24,26,28,30,0,2,4,6,8,10,12,14},{17,19,21,23,25,27,29,31,1..., dimensions={0} | all-to-all | bytes 16384 | tf_op jit(solution)/shard_map/all_to_all | solution.py:52
  117.0 8.8 %all_to_all.40.pieces_ref = f32[16,1,128]{2,1,0:T(1,128)S(1)} all-to-all(f32[16,1,128]{2,1,0:T(1,128)S(1)} %again.1), channel_id=1, replica_groups={{320,352,256,288,448,480,384,416,64,96,0,32,192,224,128,160},{321,353,2..., dimensions={0} | all-to-all | bytes 16384 | tf_op jit(solution)/shard_map/all_to_all | solution.py:52
  125.8 0.7 finished.1
  (11 shorter events, 0.1 us)
Async XLA Ops:
  2.6 9.9 %copy-start.3 = (f32[2,1,128,2,1,128]{5,4,3,2,1,0:T(1,128)S(1)}, f32[2,1,128,2,1,128]{5,4,3,2,1,0:T(1,128)}, u32[]{:S(2)}) copy-start(f32[2,1,128,2,1,128]{5,4,3,2,1,0:T(1,128)} %param.7) | copy-start | bytes 786436
  2.6 9.9 %copy-start = (f32[4,1,128,256]{3,2,1,0:T(8,128)S(1)}, f32[4,1,128,256]{3,2,1,0:T(8,128)}, u32[]{:S(2)}) copy-start(f32[4,1,128,256]{3,2,1,0:T(8,128)} %param.8) | copy-start | bytes 1572868
  2.6 24.1 %all-to-all-start = ((f32[16,128,128]{2,1,0:T(8,128)}), f32[16,128,128]{2,1,0:T(8,128)S(1)}, u32[]{:S(2)}, u32[]{:S(2)}) async-start(f32[16,128,128]{2,1,0:T(8,128)} %begin.1), calls=%async_computation | async-start | bytes 2097152 | tf_op jit(solution)/shard_map/all_to_all | solution.py:52
  12.5 0.7 copy-start.1
  12.5 0.7 copy-start.2
  13.5 6.1 %copy-start.4 = (f32[4,1,128,2,1,128]{5,4,3,2,1,0:T(1,128)S(1)}, f32[4,1,128,2,1,128]{5,4,3,2,1,0:T(1,128)}, u32[]{:S(2)}) copy-start(f32[4,1,128,2,1,128]{5,4,3,2,1,0:T(1,128)} %param.9) | copy-start | bytes 1572868
  22.2 2.3 %slice-start = ((f32[4,1,128,2,1,128]{5,4,3,2,1,0:T(1,128)}), f32[2,1,128,2,1,128]{5,4,3,2,1,0:T(1,128)S(1)}, s32[]{:S(2)}) async-start(f32[4,1,128,2,1,128]{5,4,3,2,1,0:T(1,128)} %param.6), calls=%async_computation.7 | async-start | bytes 524288 | tf_op jit(solution)/shard_map/slice | solution.py:264

commit v6 on v5

--- a/solution.py
+++ b/solution.py
@@ -103,6 +103,15 @@
 
 def picked(parts, chosen):
     return sum(jnp.dot(part, chosen, preferred_element_type=jnp.float32) for part in reversed(parts))
+
+
+def folded(left, right):
+    high, middle, low = [part.astype(jnp.float32) for part in thirds(right)]
+    wide = jnp.concatenate([merged(high, middle), merged(low, jnp.zeros_like(low))], axis=1)
+    total = picked(thirds(left), wide.astype(jnp.bfloat16))
+    lanes = right.shape[1]
+    parts = total[:, :lanes] + total[:, lanes:]
+    return parts + turned(parts)
 
 
 def across(value, core):
@@ -155,14 +164,14 @@
     values = []
     for part in range(2):
         blocks = [strided(triangle_ref, core, part * 2 * block + 1, block, 2) for core in range(2)]
-        values.append(product(jnp.concatenate(blocks, axis=1), both))
+        values.append(folded(jnp.concatenate(blocks, axis=1), both))
     sent_ref[...] = merged(*values)
 
 
 def solved(summed_ref, early_ref, inverse_ref, sent_ref, *, block):
     residual = early_ref[...] - jnp.concatenate(doubled(summed_ref[...]), axis=0)
     sent_ref[...] = merged(
-        *[product(columns_of(inverse_ref, core, 0, block), residual) for core in range(2)]
+        *[folded(columns_of(inverse_ref, core, 0, block), residual) for core in range(2)]
     )
 
 
@@ -173,7 +182,8 @@
     values = []
     for ref in (low_ref, high_ref):
         rows = ref.shape[1] // 2
-        values.append(sum(product(columns_of(ref, core, 0, rows), known[core]) for core in range(2)))
+        blocks = [columns_of(ref, core, 0, rows) for core in range(2)]
+        values.append(folded(jnp.concatenate(blocks, axis=1), jnp.concatenate(known, axis=0)))
     out = merged(*values)
     peers, stacks, rows, lanes = sent_ref.shape
     first = FIRST[LINE]

time: 129 us -> 128 us (level)
  no operation moved by 1% of the time
where the time goes in v6:
time: 128 us; the launch traced here: 126 us
  blocking collectives  110 us (86%)
  starting transfers between devices  9.84 us (8%)
  Pallas kernels  5.37 us (4%)
    all_to_all x5, blocking collectives, exchanged(): lax.all_to_all(value, axis, 0, 0, tiled=True, axis_index_groups=order)  73.2 us
    all_to_all x1, blocking collectives, to_all_pairs(): lax.all_to_all(sent, ROWS, 0, 0, tiled=True, axis_index_groups=groups)  11 us
    all_to_all x1, starting transfers between devices, exchanged(): lax.all_to_all(value, axis, 0, 0, tiled=True, axis_index_groups=order)  9.84 us
    all_gather x1, blocking collectives, shards(): both = lax.all_gather(owned, CORE)  6.9 us
    all_gather x1, blocking collectives, shards(): inverse = lax.all_gather(panel_inverse[0].reshape(-1, block), CORE)  6.13 us
    pallas_call x8, Pallas kernels, kernel(): pl.pallas_call(functools.partial(body, **settings), out_shape=outs[0] if...  5.37 us
    all_gather x1, blocking collectives, in_pairs(): return to_all_pairs(jnp.sum(lax.all_gather(value, near), axis=0))  3.78 us
  transfers between devices with their start and end apart: 1, of which 0 were waited for; matrix products, arithmetic and copies ran while one was open for 0% of the time, Pallas kernels for 0%

profile of v6, /device:TPU:1, one launch (start us, length us, event | category | flops | bytes accessed | tf_op | source)
XLA Modules:
  0.0 126.1 jit_solution(7861795145574921257)
XLA Ops:
  0.0 2.6 %begin.1 = f32[16,128,128]{2,1,0:T(8,128)} custom-call(f32[512,256]{1,0:T(8,128)} %bitcast.14, s32[1,128]{1,0:T(1,128)} %bitcast.21, s32[1,128]{1,0:T(1,128)} %bitcast.23, f32[512,128]{1,0:T(8,128)} %bitcast.28), custom_call_target="tpu_custom_call" | custom-call | tf_op jit(solution)/shard_map/begin/pallas_call | solution.py:233
  2.6 0.0 copy-start.3
  2.6 0.0 copy-start
  2.6 9.8 %all-to-all-start = ((f32[16,128,128]{2,1,0:T(8,128)}), f32[16,128,128]{2,1,0:T(8,128)S(1)}, u32[]{:S(2)}, u32[]{:S(2)}) async-start(f32[16,128,128]{2,1,0:T(8,128)} %begin.1), calls=%async_computation | async-start | bytes 2097152 | tf_op jit(solution)/shard_map/all_to_all | solution.py:52
  12.5 0.0 copy-done.3
  12.5 0.0 copy-start.1
  12.5 0.0 copy-start.2
  12.5 0.6 copy-done.1
  13.2 0.0 copy-done.2
  13.2 0.3 opening.1.early_ref
  13.5 0.0 copy-start.4
  13.5 6.1 %all_gather.30.inverse_ref = f32[2,256,128]{2,1,0:T(8,128)S(1)} all-gather(f32[1,256,128]{2,1,0:T(8,128)S(1)} %bitcast.29), channel_id=1, replica_groups=mesh['prow_0'=2,'prow_1'=2,'prow_2'=2,'prow_3'=2,'pcol_0'=16,'pcol_1'=2]..., dimensions={0}, use_global_device_ids=true | all-gather | bytes 393216 | tf_op jit(solution)/shard_map/all_gather | solution.py:273
  19.7 0.4 fusion
  20.0 2.2 %all_gather.32.low_ref = f32[2,512,128]{2,1,0:T(8,128)S(1)} all-gather(f32[1,512,128]{2,1,0:T(8,128)S(1)} %bitcast.27), channel_id=1, replica_groups=mesh['prow_0'=2,'prow_1'=2,'prow_2'=2,'prow_3'=2,'pcol_0'=16,'pcol_1'=2]..., dimensions={0}, use_global_device_ids=true | all-gather | bytes 786432 | tf_op jit(solution)/shard_map/all_gather | solution.py:275
  22.2 2.3 %all_gather.33.high_ref = f32[2,512,128]{2,1,0:T(8,128)S(1)} all-gather(f32[1,512,128]{2,1,0:T(8,128)S(1)} %bitcast.26), channel_id=1, replica_groups=mesh['prow_0'=2,'prow_1'=2,'prow_2'=2,'prow_3'=2,'pcol_0'=16,'pcol_1'=2]..., dimensions={0}, use_global_device_ids=true | all-gather | bytes 786432 | tf_op jit(solution)/shard_map/all_gather | solution.py:276
  24.5 2.2 %all_gather.31.triangle_ref = f32[2,512,128]{2,1,0:T(8,128)S(1)} all-gather(f32[1,512,128]{2,1,0:T(8,128)S(1)} %bitcast.25), channel_id=1, replica_groups=mesh['prow_0'=2,'prow_1'=2,'prow_2'=2,'prow_3'=2,'pcol_0'=16,'pcol_1'=2]..., dimensions={0}, use_global_device_ids=true | all-gather | bytes 786432 | tf_op jit(solution)/shard_map/all_gather | solution.py:274
  26.7 0.0 all-to-all-done
  26.7 0.1 reduce_sum.36
  26.8 1.9 %all-gather = f32[256,128]{1,0:T(8,128)S(1)} all-gather(f32[128,128]{1,0:T(8,128)S(1)} %reduce_sum.36), channel_id=2, replica_groups=mesh['prow_0'=2,'prow_1'=2,'prow_2'=2,'prow_3'=2,'pcol_0'=16,'pcol_1'=2]..., dimensions={0}, use_global_device_ids=true | all-gather | bytes 196608 | tf_op jit(solution)/shard_map/all_gather | solution.py:280
  28.7 0.4 coupled.1
  29.1 21.1 %all_to_all.35 = f32[16,8,128]{2,1,0:T(8,128)S(1)} all-to-all(f32[16,8,128]{2,1,0:T(8,128)S(1)} %bitcast.20), channel_id=1, replica_groups={{16,18,20,22,24,26,28,30,0,2,4,6,8,10,12,14},{17,19,21,23,25,27,29,31,1..., dimensions={0} | all-to-all | bytes 131072 | tf_op jit(solution)/shard_map/all_to_all | solution.py:52
  50.2 14.4 %all_to_all.36 = f32[16,8,128]{2,1,0:T(8,128)S(1)} all-to-all(f32[16,8,128]{2,1,0:T(8,128)S(1)} %broadcast_in_dim.4), channel_id=1, replica_groups={{16,18,20,22,24,26,28,30,0,2,4,6,8,10,12,14},{17,19,21,23,25,27,29,31,1..., dimensions={0} | all-to-all | bytes 131072 | tf_op jit(solution)/shard_map/all_to_all | solution.py:52
  64.6 0.4 solved.1
  65.1 3.8 %all-gather.1 = f32[256,128]{1,0:T(8,128)S(1)} all-gather(f32[128,128]{1,0:T(8,128)S(1)} %solved.1), channel_id=3, replica_groups=mesh['prow_0'=2,'prow_1'=2,'prow_2'=2,'prow_3'=2,'pcol_0'=16,'pcol_1'=2]..., dimensions={0}, use_global_device_ids=true | all-gather | bytes 196608 | tf_op jit(solution)/shard_map/all_gather | solution.py:61
  68.9 11.0 %all_to_all.37.pieces_ref = f32[8,128,128]{2,1,0:T(8,128)S(1)} all-to-all(f32[8,128,128]{2,1,0:T(8,128)S(1)} %broadcast_in_dim.5), channel_id=1, replica_groups={{320,288,448,416,64,32,192,160},{352,256,480,384,96,0,224,128},{321,289..., dimensions={0} | all-to-all | bytes 1048576 | tf_op jit(solution)/shard_map/all_to_all | solution.py:46
  80.0 0.8 carried.1
  80.7 16.1 %all_to_all.38 = f32[16,2,8,128]{3,2,1,0:T(8,128)S(1)} all-to-all(f32[16,2,8,128]{3,2,1,0:T(8,128)S(1)} %carried.1), channel_id=1, replica_groups={{16,18,20,22,24,26,28,30,0,2,4,6,8,10,12,14},{17,19,21,23,25,27,29,31,1..., dimensions={0} | all-to-all | bytes 262144 | tf_op jit(solution)/shard_map/all_to_all | solution.py:52
  96.8 6.9 %all-gather.2 = f32[4,8,128]{2,1,0:T(8,128)S(1)} all-gather(f32[2,8,128]{2,1,0:T(8,128)S(1)} %reduce_sum.39), channel_id=4, replica_groups=mesh['prow_0'=2,'prow_1'=2,'prow_2'=2,'prow_3'=2,'pcol_0'=16,'pcol_1'=2]..., dimensions={0}, use_global_device_ids=true | all-gather | bytes 24576 | tf_op jit(solution)/shard_map/all_gather | solution.py:295
  103.7 0.1 squared.1
  103.8 12.8 %all_to_all.39.pieces_ref = f32[16,1,128]{2,1,0:T(1,128)S(1)} all-to-all(f32[16,1,128]{2,1,0:T(1,128)S(1)} %squared.1), channel_id=1, replica_groups={{16,18,20,22,24,26,28,30,0,2,4,6,8,10,12,14},{17,19,21,23,25,27,29,31,1..., dimensions={0} | all-to-all | bytes 16384 | tf_op jit(solution)/shard_map/all_to_all | solution.py:52
  116.7 8.8 %all_to_all.40.pieces_ref = f32[16,1,128]{2,1,0:T(1,128)S(1)} all-to-all(f32[16,1,128]{2,1,0:T(1,128)S(1)} %again.1), channel_id=1, replica_groups={{320,352,256,288,448,480,384,416,64,96,0,32,192,224,128,160},{321,353,2..., dimensions={0} | all-to-all | bytes 16384 | tf_op jit(solution)/shard_map/all_to_all | solution.py:52
  125.5 0.7 finished.1
  (11 shorter events, 0.1 us)
Async XLA Ops:
  2.6 9.9 %copy-start.3 = (f32[2,1,128,2,1,128]{5,4,3,2,1,0:T(1,128)S(1)}, f32[2,1,128,2,1,128]{5,4,3,2,1,0:T(1,128)}, u32[]{:S(2)}) copy-start(f32[2,1,128,2,1,128]{5,4,3,2,1,0:T(1,128)} %param.7) | copy-start | bytes 786436
  2.6 9.9 %copy-start = (f32[4,1,128,256]{3,2,1,0:T(8,128)S(1)}, f32[4,1,128,256]{3,2,1,0:T(8,128)}, u32[]{:S(2)}) copy-start(f32[4,1,128,256]{3,2,1,0:T(8,128)} %param.8) | copy-start | bytes 1572868
  2.6 24.1 %all-to-all-start = ((f32[16,128,128]{2,1,0:T(8,128)}), f32[16,128,128]{2,1,0:T(8,128)S(1)}, u32[]{:S(2)}, u32[]{:S(2)}) async-start(f32[16,128,128]{2,1,0:T(8,128)} %begin.1), calls=%async_computation | async-start | bytes 2097152 | tf_op jit(solution)/shard_map/all_to_all | solution.py:52
  12.5 0.7 copy-start.1
  12.5 0.7 copy-start.2
  13.5 6.1 %copy-start.4 = (f32[4,1,128,2,1,128]{5,4,3,2,1,0:T(1,128)S(1)}, f32[4,1,128,2,1,128]{5,4,3,2,1,0:T(1,128)}, u32[]{:S(2)}) copy-start(f32[4,1,128,2,1,128]{5,4,3,2,1,0:T(1,128)} %param.9) | copy-start | bytes 1572868
  22.2 2.3 %slice-start = ((f32[4,1,128,2,1,128]{5,4,3,2,1,0:T(1,128)}), f32[2,1,128,2,1,128]{5,4,3,2,1,0:T(1,128)S(1)}, s32[]{:S(2)}) async-start(f32[4,1,128,2,1,128]{5,4,3,2,1,0:T(1,128)} %param.6), calls=%async_computation.7 | async-start | bytes 524288 | tf_op jit(solution)/shard_map/slice | solution.py:274

commit v7 on v6

--- a/solution.py
+++ b/solution.py
@@ -16,7 +16,7 @@
 
 EPSILON = 1e-06
 
-FIRST = {"prow_0": 1, "prow_1": 0, "prow_2": 1, "prow_3": 0, "pcol_0": 8, "pcol_1": 0}
+FIRST = {"prow_0": 1, "prow_1": 0, "prow_2": 1, "prow_3": 0, "pcol_0": 9, "pcol_1": 0}
 
 
 def product(left, right):
@@ -124,7 +124,7 @@
     sent_ref, strip_ref, targets_ref, flags_ref, inverse_ref, sems,
 ):
     panel, window = strip_ref.shape
-    block = sent_ref.shape[1]
+    block = sent_ref.shape[0]
     half = inverse_ref.shape[1]
     copies = [
         pltpu.make_async_copy(strip_hbm.at[pl.ds(panel, panel)], strip_ref, sems.at[0]),
@@ -140,9 +140,7 @@
     copies[0].wait()
     late = -picked(thirds(strip_ref[...]), chosen)
     copies[3].wait()
-    out = product(columns_of(inverse_ref, 0, 0, block), late)
-    for peer in range(sent_ref.shape[0]):
-        sent_ref[peer] = out
+    sent_ref[...] = product(columns_of(inverse_ref, 0, 0, block), late)
 
 
 def columns_of(ref, core, start, count):
@@ -157,9 +155,17 @@
     early_ref[...] = across(-picked(thirds(strip_ref[:panel, :]), chosen), core_ref[0])
 
 
-def coupled(core_ref, solved_ref, triangle_ref, sent_ref, later_ref, *, block):
-    halves = [across(solved_ref[core], core_ref[0]) for core in range(2)]
-    later_ref[...] = merged(*halves)
+def mixed(core_ref, near_ref, sent_ref):
+    sums = [near_ref[core] + near_ref[2 + core] for core in range(2)]
+    out = merged(*[across(value, core_ref[0]) for value in sums])
+    for peer in range(sent_ref.shape[0]):
+        sent_ref[peer] = out
+
+
+def coupled(pieces_ref, triangle_ref, sent_ref, later_ref, *, block):
+    later = jnp.sum(pieces_ref[...], axis=0)
+    later_ref[...] = later
+    halves = doubled(later)
     both = jnp.concatenate(halves, axis=0)
     values = []
     for part in range(2):
@@ -257,7 +263,7 @@
     paired = pair_flags.reshape(1, count)
     own_inverse = panel_inverse.reshape(-1, block)
     sent = kernel(
-        begin, [(peers, block, count)],
+        begin, [(block, count)],
         *[pltpu.with_memory_space_constraint(a, pltpu.HBM) for a in (strip, wanted, paired, own_inverse)],
         distant=4,
         scratch=(
@@ -268,20 +274,26 @@
             pltpu.SemaphoreType.DMA((4,)),
         ),
     )
-    pieces = exchanged(sent, ROWS)
+    near = lax.all_gather(sent, (ROWS[3], CORE))
+    pieces = lax.all_to_all(
+        kernel(mixed, [(peers // 2, block, count)], core, near, scalars=1),
+        ROWS, 0, 0, tiled=True, axis_index_groups=across_pairs(),
+    )
     early = kernel(opening, [(panel, count)], core, wanted, paired, strip, scalars=1)
     inverse = lax.all_gather(panel_inverse[0].reshape(-1, block), CORE)
     triangle = lax.all_gather(schur[: row_blocks // 2].reshape(-1, block), CORE)
+    pieces, early, inverse, triangle, zslab = lax.optimization_barrier(
+        (pieces, early, inverse, triangle, zslab)
+    )
+    partial_value, later = kernel(
+        coupled, [(block, count), (block, count)], pieces, triangle, block=block
+    )
+    parts = exchanged(partial_value.reshape(line, -1, count), LINE)
     low = lax.all_gather(zslab[: zrow_blocks // 2].reshape(-1, block), CORE)
     high = lax.all_gather(zslab[zrow_blocks // 2 :].reshape(-1, block), CORE)
-    pieces, early, inverse, triangle, low, high = lax.optimization_barrier(
-        (pieces, early, inverse, triangle, low, high)
-    )
-    whole = lax.all_gather(jnp.sum(pieces, axis=0), CORE)
-    partial_value, later = kernel(
-        coupled, [(block, count), (block, count)], core, whole, triangle, scalars=1, block=block
-    )
-    parts = exchanged(partial_value.reshape(line, -1, count), LINE)
+    parts, low, high = lax.optimization_barrier(
+        (parts, low, high)
+    )
     mine = jnp.sum(parts, axis=0)
     summed = exchanged(jnp.broadcast_to(mine[None], (line, *mine.shape)), LINE).reshape(block, count)
     applied = kernel(solved, [(block, count)], summed, early, inverse, block=block)

time: 128 us -> 128 us (level)
  blocking collectives: 110 us -> 97.2 us
  starting transfers between devices: 9.84 us -> 21 us
    all_to_all x5 -> x4, blocking collectives: 73.2 us -> 53.4 us  [exchanged(): lax.all_to_all(value, axis, 0, 0, tiled=True, axis_index_groups=order)]
    all_gather x1, blocking collectives: 1.91 us -> 12.5 us  [shards(): near = lax.all_gather(sent, (ROWS[3], CORE))]
    all_to_all x0 -> x1, starting transfers between devices: none -> 6.48 us  [shards(): lax.all_to_all(kernel(mixed, [(peers // 2, block, count)], core, near, sc...]
    all_to_all x1, starting transfers between devices: 9.84 us -> 14.5 us  [exchanged(): lax.all_to_all(value, axis, 0, 0, tiled=True, axis_index_groups=order)]
    all_gather x1, blocking collectives: 6.13 us -> 2.48 us  [shards(): inverse = lax.all_gather(panel_inverse[0].reshape(-1, block), CORE)]
    pallas_call x8 -> x9, Pallas kernels: 5.37 us -> 5.86 us  [kernel(): pl.pallas_call(functools.partial(body, **settings), out_shape=outs[0] if...]
  transfers between devices with their start and end apart: 1 -> 2, of which waited for: 0 -> 1; matrix products, arithmetic and copies ran while one was open for 0% -> 0% of each run, Pallas kernels for 0% -> 0%
where the time goes in v7:
time: 128 us; the launch traced here: 126 us
  blocking collectives  97.2 us (76%)
  starting transfers between devices  21 us (16%)
  Pallas kernels  5.86 us (5%)
    all_to_all x4, blocking collectives, exchanged(): lax.all_to_all(value, axis, 0, 0, tiled=True, axis_index_groups=order)  53.4 us
    all_to_all x1, starting transfers between devices, exchanged(): lax.all_to_all(value, axis, 0, 0, tiled=True, axis_index_groups=order)  14.5 us
    all_gather x1, blocking collectives, shards(): near = lax.all_gather(sent, (ROWS[3], CORE))  12.5 us
    all_to_all x1, blocking collectives, to_all_pairs(): lax.all_to_all(sent, ROWS, 0, 0, tiled=True, axis_index_groups=groups)  11.3 us
    all_to_all x1, starting transfers between devices, shards(): lax.all_to_all(kernel(mixed, [(peers // 2, block, count)], core, near, sc...  6.48 us
    all_gather x1, blocking collectives, shards(): both = lax.all_gather(owned, CORE)  6.02 us
    pallas_call x9, Pallas kernels, kernel(): pl.pallas_call(functools.partial(body, **settings), out_shape=outs[0] if...  5.86 us
    all_gather x1, blocking collectives, in_pairs(): return to_all_pairs(jnp.sum(lax.all_gather(value, near), axis=0))  3.78 us
  transfers between devices with their start and end apart: 2, of which 1 were waited for; matrix products, arithmetic and copies ran while one was open for 0% of the time, Pallas kernels for 0%

profile of v7, /device:TPU:1, one launch (start us, length us, event | category | flops | bytes accessed | tf_op | source)
XLA Modules:
  0.0 126.0 jit_solution(1427885501083131140)
XLA Ops:
  0.0 1.5 %begin.1 = f32[128,128]{1,0:T(8,128)S(1)} custom-call(f32[512,256]{1,0:T(8,128)} %bitcast.14, s32[1,128]{1,0:T(1,128)} %bitcast.20, s32[1,128]{1,0:T(1,128)} %bitcast.22, f32[512,128]{1,0:T(8,128)} %bitcast.27), custom_call_target="tpu_custom_call" | custom-call | tf_op jit(solution)/shard_map/begin/pallas_call | solution.py:239
  1.6 12.5 %all-gather = f32[512,128]{1,0:T(8,128)S(1)} all-gather(f32[128,128]{1,0:T(8,128)S(1)} %begin.1), channel_id=2, replica_groups=mesh['prow_0'=2,'prow_1'=2,'prow_2'=2,'prow_3'=2,'pcol_0'=16,'pcol_1'=2]..., dimensions={0}, use_global_device_ids=true | all-gather | bytes 327680 | tf_op jit(solution)/shard_map/all_gather | solution.py:277
  14.0 0.9 mixed.1
  14.9 6.5 %all-to-all-start = ((f32[8,128,128]{2,1,0:T(8,128)}), f32[8,128,128]{2,1,0:T(8,128)S(1)}, u32[]{:S(2)}, u32[]{:S(2)}) async-start(f32[8,128,128]{2,1,0:T(8,128)} %mixed.1), calls=%async_computation | async-start | bytes 1048576 | tf_op jit(solution)/shard_map/all_to_all | solution.py:278
  21.4 0.0 copy-done
  21.4 0.0 copy-done.1
  21.4 0.0 copy-done.2
  21.4 0.0 copy-start.3
  21.5 0.3 opening.1.early_ref
  21.8 0.6 copy-done.3
  22.4 0.0 slice-start
  22.4 2.5 %all_gather.32.inverse_ref = f32[2,256,128]{2,1,0:T(8,128)S(1)} all-gather(f32[1,256,128]{2,1,0:T(8,128)S(1)} %bitcast.28), channel_id=1, replica_groups=mesh['prow_0'=2,'prow_1'=2,'prow_2'=2,'prow_3'=2,'pcol_0'=16,'pcol_1'=2]..., dimensions={0}, use_global_device_ids=true | all-gather | bytes 393216 | tf_op jit(solution)/shard_map/all_gather | solution.py:283
  24.9 0.0 slice-done
  24.9 2.2 %all_gather.33.triangle_ref = f32[2,512,128]{2,1,0:T(8,128)S(1)} all-gather(f32[1,512,128]{2,1,0:T(8,128)S(1)} %bitcast.24), channel_id=1, replica_groups=mesh['prow_0'=2,'prow_1'=2,'prow_2'=2,'prow_3'=2,'pcol_0'=16,'pcol_1'=2]..., dimensions={0}, use_global_device_ids=true | all-gather | bytes 786432 | tf_op jit(solution)/shard_map/all_gather | solution.py:284
  27.1 0.8 all-to-all-done.pieces_ref
  27.9 1.1 coupled.1
  28.9 14.5 %all-to-all-start.1 = ((f32[16,8,128]{2,1,0:T(8,128)}), f32[16,8,128]{2,1,0:T(8,128)S(1)}, u32[]{:S(2)}, u32[]{:S(2)}) async-start(f32[16,8,128]{2,1,0:T(8,128)} %bitcast.8), calls=%async_computation.1 | async-start | bytes 131072 | tf_op jit(solution)/shard_map/all_to_all | solution.py:52
  43.4 0.4 fusion
  43.8 3.4 %all_gather.34.low_ref = f32[2,512,128]{2,1,0:T(8,128)S(1)} all-gather(f32[1,512,128]{2,1,0:T(8,128)S(1)} %bitcast.26), channel_id=1, replica_groups=mesh['prow_0'=2,'prow_1'=2,'prow_2'=2,'prow_3'=2,'pcol_0'=16,'pcol_1'=2]..., dimensions={0}, use_global_device_ids=true | all-gather | bytes 786432 | tf_op jit(solution)/shard_map/all_gather | solution.py:292
  47.2 2.2 %all_gather.35.high_ref = f32[2,512,128]{2,1,0:T(8,128)S(1)} all-gather(f32[1,512,128]{2,1,0:T(8,128)S(1)} %bitcast.25), channel_id=1, replica_groups=mesh['prow_0'=2,'prow_1'=2,'prow_2'=2,'prow_3'=2,'pcol_0'=16,'pcol_1'=2]..., dimensions={0}, use_global_device_ids=true | all-gather | bytes 786432 | tf_op jit(solution)/shard_map/all_gather | solution.py:293
  49.4 0.0 all-to-all-done.1
  49.4 15.8 %all_to_all.35 = f32[16,8,128]{2,1,0:T(8,128)S(1)} all-to-all(f32[16,8,128]{2,1,0:T(8,128)S(1)} %broadcast_in_dim.4), channel_id=1, replica_groups={{18,20,22,24,26,28,30,0,2,4,6,8,10,12,14,16},{19,21,23,25,27,29,31,1,3,..., dimensions={0} | all-to-all | bytes 131072 | tf_op jit(solution)/shard_map/all_to_all | solution.py:52
  65.2 0.4 solved.1
  65.6 3.8 %all-gather.1 = f32[256,128]{1,0:T(8,128)S(1)} all-gather(f32[128,128]{1,0:T(8,128)S(1)} %solved.1), channel_id=3, replica_groups=mesh['prow_0'=2,'prow_1'=2,'prow_2'=2,'prow_3'=2,'pcol_0'=16,'pcol_1'=2]..., dimensions={0}, use_global_device_ids=true | all-gather | bytes 196608 | tf_op jit(solution)/shard_map/all_gather | solution.py:61
  69.5 11.3 %all_to_all.36.pieces_ref = f32[8,128,128]{2,1,0:T(8,128)S(1)} all-to-all(f32[8,128,128]{2,1,0:T(8,128)S(1)} %broadcast_in_dim.5), channel_id=1, replica_groups={{320,288,448,416,64,32,192,160},{352,256,480,384,96,0,224,128},{321,289..., dimensions={0} | all-to-all | bytes 1048576 | tf_op jit(solution)/shard_map/all_to_all | solution.py:46
  80.8 0.8 carried.1
  81.5 16.0 %all_to_all.37 = f32[16,2,8,128]{3,2,1,0:T(8,128)S(1)} all-to-all(f32[16,2,8,128]{3,2,1,0:T(8,128)S(1)} %carried.1), channel_id=1, replica_groups={{18,20,22,24,26,28,30,0,2,4,6,8,10,12,14,16},{19,21,23,25,27,29,31,1,3,..., dimensions={0} | all-to-all | bytes 262144 | tf_op jit(solution)/shard_map/all_to_all | solution.py:52
  97.6 6.0 %all-gather.2 = f32[4,8,128]{2,1,0:T(8,128)S(1)} all-gather(f32[2,8,128]{2,1,0:T(8,128)S(1)} %reduce_sum.29), channel_id=4, replica_groups=mesh['prow_0'=2,'prow_1'=2,'prow_2'=2,'prow_3'=2,'pcol_0'=16,'pcol_1'=2]..., dimensions={0}, use_global_device_ids=true | all-gather | bytes 24576 | tf_op jit(solution)/shard_map/all_gather | solution.py:307
  103.6 0.1 squared.1
  103.7 12.8 %all_to_all.38.pieces_ref = f32[16,1,128]{2,1,0:T(1,128)S(1)} all-to-all(f32[16,1,128]{2,1,0:T(1,128)S(1)} %squared.1), channel_id=1, replica_groups={{18,20,22,24,26,28,30,0,2,4,6,8,10,12,14,16},{19,21,23,25,27,29,31,1,3,..., dimensions={0} | all-to-all | bytes 16384 | tf_op jit(solution)/shard_map/all_to_all | solution.py:52
  116.5 8.8 %all_to_all.39.pieces_ref = f32[16,1,128]{2,1,0:T(1,128)S(1)} all-to-all(f32[16,1,128]{2,1,0:T(1,128)S(1)} %again.1), channel_id=1, replica_groups={{320,352,256,288,448,480,384,416,64,96,0,32,192,224,128,160},{321,353,2..., dimensions={0} | all-to-all | bytes 16384 | tf_op jit(solution)/shard_map/all_to_all | solution.py:52
  125.3 0.7 finished.1
  (12 shorter events, 0.1 us)
Async XLA Ops:
  14.9 6.5 %copy-start = (f32[4,1,128,256]{3,2,1,0:T(8,128)S(1)}, f32[4,1,128,256]{3,2,1,0:T(8,128)}, u32[]{:S(2)}) copy-start(f32[4,1,128,256]{3,2,1,0:T(8,128)} %param.8) | copy-start | bytes 1572868
  14.9 6.5 %copy-start.1 = (s32[128]{0:T(128)S(1)}, s32[128]{0:T(128)}, u32[]{:S(2)}) copy-start(s32[128]{0:T(128)} %param.10) | copy-start | bytes 1540
  14.9 6.5 %copy-start.2 = (s32[128]{0:T(128)S(1)}, s32[128]{0:T(128)}, u32[]{:S(2)}) copy-start(s32[128]{0:T(128)} %param.11) | copy-start | bytes 1540
  14.9 12.9 %all-to-all-start = ((f32[8,128,128]{2,1,0:T(8,128)}), f32[8,128,128]{2,1,0:T(8,128)S(1)}, u32[]{:S(2)}, u32[]{:S(2)}) async-start(f32[8,128,128]{2,1,0:T(8,128)} %mixed.1), calls=%async_computation | async-start | bytes 1048576 | tf_op jit(solution)/shard_map/all_to_all | solution.py:278
  21.4 1.0 copy-start.3
  22.4 2.5 %slice-start = ((f32[4,1,128,2,1,128]{5,4,3,2,1,0:T(1,128)}), f32[2,1,128,2,1,128]{5,4,3,2,1,0:T(1,128)S(1)}, s32[]{:S(2)}) async-start(f32[4,1,128,2,1,128]{5,4,3,2,1,0:T(1,128)} %param.6), calls=%async_computation.7 | async-start | bytes 524288 | tf_op jit(solution)/shard_map/slice | solution.py:284
  27.1 16.4 %copy-start.4 = (f32[4,1,128,2,1,128]{5,4,3,2,1,0:T(1,128)S(1)}, f32[4,1,128,2,1,128]{5,4,3,2,1,0:T(1,128)}, u32[]{:S(2)}) copy-start(f32[4,1,128,2,1,128]{5,4,3,2,1,0:T(1,128)} %param.9) | copy-start | bytes 1572868
  28.9 20.4 %all-to-all-start.1 = ((f32[16,8,128]{2,1,0:T(8,128)}), f32[16,8,128]{2,1,0:T(8,128)S(1)}, u32[]{:S(2)}, u32[]{:S(2)}) async-start(f32[16,8,128]{2,1,0:T(8,128)} %bitcast.8), calls=%async_computation.1 | async-start | bytes 131072 | tf_op jit(solution)/shard_map/all_to_all | solution.py:52
